TPU v7x, 512 devices: a 4x2x32 block of a 4x8x32 slice. The times are simulated.
512 devices in a mesh: groups: 2 (over y), grid: 32 (over z), row: 2 (over core), rep: 4 (over x).
Axes of the slice: x: 4, y: 2, z: 32, core: 2. Of those that a mesh axis runs over, the one named last changes fastest.
The devices are a block of a 4x8x32 slice.
Arguments:
- tokens: bfloat16 [2048, 4096], P(('groups', 'grid', 'rep'), 'row'), parts along dimension 0, may hold values from -40 to 40
- target_tokens: int32 [2048], P('groups'), parts along dimension 0, may hold values from 0 to 31999
- gate_weight: bfloat16 [4096, 14336], P(('row', 'rep'), 'grid'), may hold values from -0.09375 to 0.09375
- up_weight: bfloat16 [4096, 14336], P(('row', 'rep'), 'grid'), may hold values from -0.09375 to 0.09375
- down_weight: bfloat16 [14336, 4096], P('grid', ('row', 'rep')), may hold values from -0.046875 to 0.046875
- norm_gain: float32 [4096], P('row'), may hold values from 0.5 to 1.5
- vocab_weight: bfloat16 [4096, 32000], P('row', ('grid', 'rep')), may hold values from -6 to 6
Outputs:
- mixed: bfloat16 [2048, 4096], P(('groups', 'grid', 'rep'), 'row'), parts along dimension 0
- logprob: float32 [2048], P(('groups', 'grid', 'rep')), parts along dimension 0
There are 2 independent parts, one for each index of `groups`. A program takes and returns all parts, laid end to end along the dimension named above; an argument that names none is the same for every part. Nothing has to cross between parts.
All inputs are finite; a program needn't handle non-finite values.
Results may differ from a plain program's by a relative error of at most 0.0046.
Values may be sent and summed in bfloat16 or wider, within the bound.
No kernel may reach another device: no remote copies, remote signals or barrier semaphores. Data moves between devices by JAX's collectives and lax.ppermute only.
A program may use at most 64 MiB of HBM per device.

v0:
```python
import jax
import jax.numpy as jnp
from jax import lax
from jax.sharding import PartitionSpec as P

GATE_UP_REACH = 0.09375
DOWN_REACH = 0.046875


def parity_groups(size):
    return [list(range(side, size, 2)) for side in (0, 1)]


def swapped_in_pairs(value, axis):
    size = lax.axis_size(axis)
    return lax.ppermute(value, axis, [(i, i ^ 1) for i in range(size)])


def sent_to_all(value, axis):
    peers = lax.axis_size(axis)
    return lax.all_to_all(
        jnp.broadcast_to(value[None], (peers, *value.shape)), axis, 0, 0, tiled=True
    )


def shifted(value, axis, step):
    size = lax.axis_size(axis)
    return lax.ppermute(value, axis, [(i, (i + step) % size) for i in range(size)])


def placed(parts, axis, size):
    out = jnp.broadcast_to(parts[0][None], (size, *parts[0].shape))
    for step, value, first_row in parts[1:]:
        place = lax.rem(lax.axis_index(axis) + (step + size), size)
        out = lax.dynamic_update_slice(out, value[None], (place, first_row, 0))
    return out


def both_halves(part, axis):
    return part + lax.ppermute(part, axis, [(0, 1), (1, 0)])


def hidden_units(rows, blocks, width):
    features = blocks.shape[2]
    part = sum(
        lax.dot_general(
            rows[:, k * features : (k + 1) * features],
            blocks[k, :width],
            (((1,), (1,)), ((), ())),
            preferred_element_type=jnp.float32,
        )
        for k in range(blocks.shape[0])
    )
    value = both_halves(part, "row")
    gate_value, up_value = jnp.split(value, 2, axis=1)
    return (jax.nn.silu(gate_value) * up_value).astype(jnp.bfloat16)


def projected(hidden, blocks, width):
    out = [
        jnp.dot(hidden, blocks[k, width:], preferred_element_type=jnp.float32)
        for k in range(blocks.shape[0])
    ]
    return jnp.concatenate(out, axis=1)


def row_stats(normed, weights, targets, column_start):
    part = jnp.einsum("tk,rkv->rtv", normed, weights, preferred_element_type=jnp.float32)
    logits = both_halves(part, "row")
    ids = lax.broadcasted_iota(jnp.int32, logits.shape, 0) * logits.shape[2] + lax.broadcasted_iota(
        jnp.int32, logits.shape, 2
    )
    top = jnp.max(logits, axis=(0, 2))
    total = jnp.sum(jnp.exp(logits - top[None, :, None]), axis=(0, 2))
    picked = jnp.sum(
        jnp.where(ids == (targets - column_start)[None, :, None], logits, 0.0), axis=(0, 2)
    )
    return jnp.stack([top, total, picked])


def device_step(tokens, target_tokens, gate_weight, up_weight, down_weight, norm_gain, vocab_weight):
    own_rows, half_width = tokens.shape
    features = half_width * lax.axis_size("row")
    grid = lax.axis_size("grid")
    rep = lax.axis_size("rep")
    side = lax.rem(lax.axis_index("grid"), 2)

    block = jnp.concatenate([gate_weight.T, up_weight.T, down_weight], axis=0)
    after = shifted(block, "rep", -1)
    before = shifted(block, "rep", 1)
    width = gate_weight.shape[1] + up_weight.shape[1]

    own = lax.all_gather(tokens, "grid", axis=0, axis_index_groups=parity_groups(grid))
    own = own.reshape(-1, half_width)
    own, after_held, before_held = lax.optimization_barrier((own, after, before))
    middle = block.shape[0] // 2
    far_first = shifted(after_held[:middle], "rep", -1)
    far_last = shifted(before_held[middle:], "rep", 1)
    other = swapped_in_pairs(own, "grid")
    vocab = sent_to_all(vocab_weight, "rep")
    blocks = placed(
        [block, (1, after_held, 0), (-1, before_held, 0), (2, far_first, 0), (2, far_last, middle)],
        "rep",
        rep,
    )
    rows = jnp.concatenate([other, own], axis=0)
    length = lax.psum(jnp.sum(jnp.abs(rows.astype(jnp.float32)), axis=1), "row")
    units = down_weight.shape[0] * grid
    reach = jnp.maximum(jnp.square(GATE_UP_REACH * length) * (DOWN_REACH * units), 1e-20) / 30000.0
    share = (1.0 / reach)[:, None]
    half = own.shape[0]

    hidden = hidden_units(rows, blocks, width)
    branch_other = (projected(hidden[:half], blocks, width) * share[:half]).astype(jnp.float16)
    arrived = swapped_in_pairs(branch_other, "grid")
    branch_own = projected(hidden[half:], blocks, width) * share[half:]
    pair_sum = (branch_own + arrived.astype(jnp.float32)).astype(jnp.float16)
    branch = lax.psum(pair_sum, "grid", axis_index_groups=parity_groups(grid))
    mixed_own = (own.astype(jnp.float32) + branch.astype(jnp.float32) * reach[half:, None]).astype(
        jnp.bfloat16
    )
    mixed = lax.dynamic_slice_in_dim(mixed_own, lax.div(lax.axis_index("grid"), 2) * own_rows, own_rows, 0)
    held = lax.optimization_barrier(mixed_own).astype(jnp.float32)
    squares = lax.psum(jnp.sum(held * held, axis=1), "row")
    scale = lax.rsqrt(squares / features + 1e-05)
    normed_own = (held * scale[:, None] * norm_gain[None, :]).astype(jnp.bfloat16)
    normed_other = swapped_in_pairs(normed_own, "grid")
    targets = lax.dynamic_slice_in_dim(
        target_tokens.reshape(grid // 2, 2, rep, own_rows), lax.axis_index("rep"), 1, 2
    )[:, :, 0]
    targets_own = lax.dynamic_slice_in_dim(targets, side, 1, 1).reshape(-1)
    targets_other = lax.dynamic_slice_in_dim(targets, 1 - side, 1, 1).reshape(-1)
    column_start = lax.axis_index("grid") * (vocab.shape[0] * vocab.shape[2])
    stats_own = row_stats(normed_own, vocab, targets_own, column_start)
    stats_other = row_stats(normed_other, vocab, targets_other, column_start)
    pieces = jnp.stack([stats_own, stats_other])
    pieces = jnp.where(side == 0, pieces, pieces[::-1]).reshape(2, 3, grid // 2, own_rows)
    pieces = pieces.transpose(2, 0, 1, 3).reshape(grid, 3 * own_rows)
    found = lax.all_to_all(pieces, "grid", 0, 0, tiled=True).reshape(grid, 3, own_rows)
    top = jnp.max(found[:, 0], axis=0)
    total = jnp.sum(found[:, 1] * jnp.exp(found[:, 0] - top[None]), axis=0)
    logprob = jnp.sum(found[:, 2], axis=0) - top - jnp.log(total)
    return (mixed, logprob)


def solution(mesh):
    in_specs = (
        P(("groups", "grid", "rep"), "row"),
        P("groups"),
        P(("row", "rep"), "grid"),
        P(("row", "rep"), "grid"),
        P("grid", ("row", "rep")),
        P("row"),
        P("row", ("grid", "rep")),
    )
    out_specs = (P(("groups", "grid", "rep"), "row"), P(("groups", "grid", "rep")))
    return jax.shard_map(
        device_step, mesh=mesh, in_specs=in_specs, out_specs=out_specs, check_vma=False
    )
```

profile of v0, /device:TPU:40, one launch (start us, length us, event | category | flops | bytes accessed | tf_op | source)
XLA Modules:
  0.0 274.5 jit_solution(6892463300301543265)
XLA Ops:
  0.6 1.4 pad_maximum_fusion
  2.0 5.1 %collective-permute-start = (bf16[1344,512]{1,0:T(8,128)(2,1)S(1)}, bf16[1344,512]{1,0:T(8,128)(2,1)S(1)}, u32[]{:S(2)}, u32[]{:S(2)}) collective-permute-start(bf16[1344,512]{1,0:T(8,128)(2,1)S(1)} %pad_maximum_fusion), channel_id=1, source_target_pairs={{0,3},{1,0},{2,1},{3,2},{4,7},{5,4},{6,5},{7,6},{8,11},{9,8},{10,9... | collective-permute-start | bytes 4128776 | tf_op jit(solution)/shard_map/ppermute | solution.py:28
  7.1 2.0 collective-permute-start.1
  9.1 76.4 %all-gather = bf16[128,2048]{1,0:T(8,128)(2,1)S(1)} all-gather(bf16[8,2048]{1,0:T(8,128)(2,1)} %param.7), channel_id=2, replica_groups={{0,16,32,48,64,80,96,112,128,144,160,176,192,208,224,240},{8,24,40,56,7..., dimensions={0}, use_global_device_ids=true | all-gather | bytes 557056 | tf_op jit(solution)/shard_map/all_gather | solution.py:93
  85.6 4.9 %collective-permute-start.3 = (bf16[672,512]{1,0:T(8,128)(2,1)S(1)}, bf16[672,512]{1,0:T(8,128)(2,1)S(1)}, u32[]{:S(2)}, u32[]{:S(2)}) collective-permute-start(bf16[672,512]{1,0:T(8,128)(2,1)S(1)} %slice.74), channel_id=1, source_target_pairs={{0,3},{1,0},{2,1},{3,2},{4,7},{5,4},{6,5},{7,6},{8,11},{9,8},{10,9... | collective-permute-start | bytes 2064392 | tf_op jit(solution)/shard_map/ppermute | solution.py:28
  90.5 1.1 slice.75
  91.7 2.0 collective-permute-start.4
  93.6 3.8 %collective-permute-start.2 = (bf16[128,2048]{1,0:T(8,128)(2,1)S(1)}, bf16[128,2048]{1,0:T(8,128)(2,1)S(1)}, u32[]{:S(2)}, u32[]{:S(2)}) collective-permute-start(bf16[128,2048]{1,0:T(8,128)(2,1)S(1)} %all-gather), channel_id=1, source_target_pairs={{0,8},{8,0},{16,24},{24,16},{32,40},{40,32},{48,56},{56,48},{64,72... | collective-permute-start | bytes 1572872 | tf_op jit(solution)/shard_map/ppermute | solution.py:16
  97.4 0.4 broadcast_in_dim.16
  97.9 0.1 bitcast_dynamic-update-slice_fusion.1
  98.0 1.5 bitcast_dynamic-update-slice_fusion
  99.5 5.3 %collective-permute-done.2 = bf16[128,2048]{1,0:T(8,128)(2,1)S(1)} collective-permute-done((bf16[128,2048]{1,0:T(8,128)(2,1)S(1)}, bf16[128,2048]{1,0:T(8,128)(2,1)S(1)}, u32[]{:S(2)}, u32[]{:S(2)}) %collective-permute-start.2) | collective-permute-done | bytes 524320 | tf_op jit(solution)/shard_map/ppermute | solution.py:16
  104.9 0.8 collective-permute-done.4
  105.8 0.5 fusion.10
  106.3 0.5 fusion.9
  106.8 0.5 fusion.8
  107.2 0.5 fusion.1
  107.7 0.5 copy-done
  108.2 1.9 collective-permute-start.5
  110.2 2.4 broadcast_in_dim.22
  112.5 5.0 %all-to-all-start = ((bf16[4,2048,250]{2,1,0:T(8,128)(2,1)}), bf16[4,2048,250]{2,1,0:T(8,128)(2,1)}, u32[]{:S(2)}, u32[]{:S(2)}) async-start(bf16[4,2048,250]{2,1,0:T(8,128)(2,1)} %broadcast_in_dim.22), calls=%async_computation | async-start | bytes 8388608 | tf_op jit(solution)/shard_map/all_to_all | solution.py:21
  117.5 0.3 abs_reduce_fusion
  117.8 2.7 psum.21
  120.5 1.4 add.96
  121.9 0.2 fusion.11
  122.1 1.5 fusion.16
  123.6 1.2 fusion.18
  124.9 0.2 fusion.20
  125.1 0.2 fusion.22
  125.3 0.2 fusion.17
  125.6 0.2 fusion.7
  125.7 3.8 %collective-permute-start.6 = (f16[128,2048]{1,0:T(8,128)(2,1)S(1)}, f16[128,2048]{1,0:T(8,128)(2,1)S(1)}, u32[]{:S(2)}, u32[]{:S(2)}) collective-permute-start(f16[128,2048]{1,0:T(8,128)(2,1)S(1)} %fusion.7), channel_id=1, source_target_pairs={{0,8},{8,0},{16,24},{24,16},{32,40},{40,32},{48,56},{56,48},{64,72... | collective-permute-start | bytes 1572872 | tf_op jit(solution)/shard_map/ppermute | solution.py:16
  129.5 0.2 fusion.19
  129.7 0.2 fusion.21
  130.0 0.2 fusion.23
  130.2 11.7 %collective-permute-done.6 = f16[128,2048]{1,0:T(8,128)(2,1)S(1)} collective-permute-done((f16[128,2048]{1,0:T(8,128)(2,1)S(1)}, f16[128,2048]{1,0:T(8,128)(2,1)S(1)}, u32[]{:S(2)}, u32[]{:S(2)}) %collective-permute-start.6) | collective-permute-done | bytes 524320 | tf_op jit(solution)/shard_map/ppermute | solution.py:16
  141.9 0.2 fusion.6
  142.2 68.3 %all-reduce.1 = u32[4,32768]{1,0:T(4,128)S(1)} all-reduce(u32[4,32768]{1,0:T(4,128)S(1)} %bitcast.79), channel_id=1, replica_groups={{0,16,32,48,64,80,96,112,128,144,160,176,192,208,224,240},{8,24,40,56,7..., use_global_device_ids=true, to_apply=%region_2.3.clone | all-reduce | flops 131072 | bytes 1048576 | tf_op jit(solution)/shard_map/psum | solution.py:118
  210.4 0.2 add_convert_fusion
  210.7 0.2 fusion.2
  210.9 2.5 psum.23
  213.4 0.2 fusion.4
  213.6 4.6 %collective-permute-start.8 = (bf16[128,2048]{1,0:T(8,128)(2,1)S(1)}, bf16[128,2048]{1,0:T(8,128)(2,1)S(1)}, u32[]{:S(2)}, u32[]{:S(2)}) collective-permute-start(bf16[128,2048]{1,0:T(8,128)(2,1)S(1)} %fusion.4), channel_id=1, source_target_pairs={{0,8},{8,0},{16,24},{24,16},{32,40},{40,32},{48,56},{56,48},{64,72... | collective-permute-start | bytes 1572872 | tf_op jit(solution)/shard_map/ppermute | solution.py:16
  218.2 2.9 %convolution_bitcast_fusion.1 = f32[4,128,250]{2,1,0:T(8,128)S(1)} fusion(bf16[4,2048,250]{2,1,0:T(8,128)(2,1)} %all-to-all-done, bf16[128,2048]{1,0:T(8,128)(2,1)S(1)} %fusion.4), kind=kOutput, calls=%fused_computation.10 | convolution fusion | flops 524288000 | bytes 5132288 | tf_op jit(solution)/shard_map/tk,rkv->rtv/dot_general | solution.py:68
  221.1 2.0 collective-permute-start.7
  223.1 7.4 %collective-permute-done.8 = bf16[128,2048]{1,0:T(8,128)(2,1)S(1)} collective-permute-done((bf16[128,2048]{1,0:T(8,128)(2,1)S(1)}, bf16[128,2048]{1,0:T(8,128)(2,1)S(1)}, u32[]{:S(2)}, u32[]{:S(2)}) %collective-permute-start.8) | collective-permute-done | bytes 524320 | tf_op jit(solution)/shard_map/ppermute | solution.py:16
  230.4 2.9 %convolution_bitcast_fusion = f32[4,128,250]{2,1,0:T(8,128)S(1)} fusion(bf16[4,2048,250]{2,1,0:T(8,128)(2,1)} %all-to-all-done, bf16[128,2048]{1,0:T(8,128)(2,1)S(1)} %collective-permute-done.8), kind=kOutput, calls=%fused_computation.9 | convolution fusion | flops 524288000 | bytes 5132288 | tf_op jit(solution)/shard_map/tk,rkv->rtv/dot_general | solution.py:68
  233.3 2.0 collective-permute-start.9
  235.3 0.1 reshape.54
  235.5 0.1 sub.61
  235.6 0.1 sub.66
  235.7 0.1 fusion.39
  235.9 1.3 collective-permute-done.9
  237.2 0.1 fusion.40
  237.3 0.4 exponential_reduce_fusion.1
  237.8 0.1 reshape.55
  237.9 0.7 all_to_all.10
  238.6 13.3 %all-to-all-start.1 = ((f32[32,1,24]{2,1,0:T(1,128)}), f32[32,1,24]{2,1,0:T(1,128)S(1)}, u32[]{:S(2)}, u32[]{:S(2)}) async-start(f32[32,1,24]{2,1,0:T(1,128)} %bitcast.27), calls=%async_computation.1 | async-start | bytes 32768 | tf_op jit(solution)/shard_map/all_to_all | solution.py:139
  251.9 0.6 constant_dynamic-slice_fusion
  252.5 21.0 %all-to-all-done.1 = f32[32,1,24]{2,1,0:T(1,128)S(1)} async-done(((f32[32,1,24]{2,1,0:T(1,128)}), f32[32,1,24]{2,1,0:T(1,128)S(1)}, u32[]{:S(2)}, u32[]{:S(2)}) %all-to-all-start.1) | async-done | bytes 3104 | tf_op jit(solution)/shard_map/all_to_all | solution.py:139
  273.6 0.1 copy.16
  273.6 0.2 slice_reduce_fusion
  273.8 0.2 fusion.37
  274.0 0.5 log_subtract_fusion
  (31 shorter events, 0.4 us)
Async XLA Ops:
  2.0 83.5 %collective-permute-start = (bf16[1344,512]{1,0:T(8,128)(2,1)S(1)}, bf16[1344,512]{1,0:T(8,128)(2,1)S(1)}, u32[]{:S(2)}, u32[]{:S(2)}) collective-permute-start(bf16[1344,512]{1,0:T(8,128)(2,1)S(1)} %pad_maximum_fusion), channel_id=1, source_target_pairs={{0,3},{1,0},{2,1},{3,2},{4,7},{5,4},{6,5},{7,6},{8,11},{9,8},{10,9... | collective-permute-start | bytes 4128776 | tf_op jit(solution)/shard_map/ppermute | solution.py:28
  7.1 78.4 %collective-permute-start.1 = (bf16[1344,512]{1,0:T(8,128)(2,1)S(1)}, bf16[1344,512]{1,0:T(8,128)(2,1)}, u32[]{:S(2)}, u32[]{:S(2)}) collective-permute-start(bf16[1344,512]{1,0:T(8,128)(2,1)S(1)} %pad_maximum_fusion), channel_id=1, source_target_pairs={{0,1},{1,2},{2,3},{3,0},{4,5},{5,6},{6,7},{7,4},{8,9},{9,10},{10,1... | collective-permute-start | bytes 4128776 | tf_op jit(solution)/shard_map/ppermute | solution.py:28
  85.6 19.3 %collective-permute-start.3 = (bf16[672,512]{1,0:T(8,128)(2,1)S(1)}, bf16[672,512]{1,0:T(8,128)(2,1)S(1)}, u32[]{:S(2)}, u32[]{:S(2)}) collective-permute-start(bf16[672,512]{1,0:T(8,128)(2,1)S(1)} %slice.74), channel_id=1, source_target_pairs={{0,3},{1,0},{2,1},{3,2},{4,7},{5,4},{6,5},{7,6},{8,11},{9,8},{10,9... | collective-permute-start | bytes 2064392 | tf_op jit(solution)/shard_map/ppermute | solution.py:28
  91.7 14.1 %collective-permute-start.4 = (bf16[672,512]{1,0:T(8,128)(2,1)S(1)}, bf16[672,512]{1,0:T(8,128)(2,1)S(1)}, u32[]{:S(2)}, u32[]{:S(2)}) collective-permute-start(bf16[672,512]{1,0:T(8,128)(2,1)S(1)} %slice.75), channel_id=1, source_target_pairs={{0,1},{1,2},{2,3},{3,0},{4,5},{5,6},{6,7},{7,4},{8,9},{9,10},{10,1... | collective-permute-start | bytes 2064392 | tf_op jit(solution)/shard_map/ppermute | solution.py:28
  93.6 11.1 %collective-permute-start.2 = (bf16[128,2048]{1,0:T(8,128)(2,1)S(1)}, bf16[128,2048]{1,0:T(8,128)(2,1)S(1)}, u32[]{:S(2)}, u32[]{:S(2)}) collective-permute-start(bf16[128,2048]{1,0:T(8,128)(2,1)S(1)} %all-gather), channel_id=1, source_target_pairs={{0,8},{8,0},{16,24},{24,16},{32,40},{40,32},{48,56},{56,48},{64,72... | collective-permute-start | bytes 1572872 | tf_op jit(solution)/shard_map/ppermute | solution.py:16
  105.8 2.4 copy-start
  105.8 4.3 %copy-start.2 = (bf16[2048,250]{1,0:T(8,128)(2,1)S(1)}, bf16[2048,250]{1,0:T(8,128)(2,1)}, u32[]{:S(2)}) copy-start(bf16[2048,250]{1,0:T(8,128)(2,1)} %param.13) | copy-start | bytes 3072004
  108.2 12.3 %collective-permute-start.5 = (f32[256,896]{1,0:T(8,128)S(1)}, f32[256,896]{1,0:T(8,128)}, u32[]{:S(2)}, u32[]{:S(2)}) collective-permute-start(f32[256,896]{1,0:T(8,128)S(1)} %fusion.1), channel_id=1, source_target_pairs={{0,4},{4,0},{1,5},{5,1},{2,6},{6,2},{3,7},{7,3},{8,12},{12,8},{9,1... | collective-permute-start | bytes 2752520 | tf_op jit(solution)/shard_map/ppermute | solution.py:40
  112.5 105.7 %all-to-all-start = ((bf16[4,2048,250]{2,1,0:T(8,128)(2,1)}), bf16[4,2048,250]{2,1,0:T(8,128)(2,1)}, u32[]{:S(2)}, u32[]{:S(2)}) async-start(bf16[4,2048,250]{2,1,0:T(8,128)(2,1)} %broadcast_in_dim.22), calls=%async_computation | async-start | bytes 8388608 | tf_op jit(solution)/shard_map/all_to_all | solution.py:21
  120.5 4.4 %copy-start.1 = (bf16[4,1344,512]{2,1,0:T(8,128)(2,1)S(1)}, bf16[4,1344,512]{2,1,0:T(8,128)(2,1)}, u32[]{:S(2)}) copy-start(bf16[4,1344,512]{2,1,0:T(8,128)(2,1)} %copy-done) | copy-start | bytes 16515076
  125.1 88.3 %copy-start.3 = (f32[2048]{0:T(1024)S(1)}, f32[2048]{0:T(1024)}, u32[]{:S(2)}) copy-start(f32[2048]{0:T(1024)} %param.12) | copy-start | bytes 24580
  125.7 16.2 %collective-permute-start.6 = (f16[128,2048]{1,0:T(8,128)(2,1)S(1)}, f16[128,2048]{1,0:T(8,128)(2,1)S(1)}, u32[]{:S(2)}, u32[]{:S(2)}) collective-permute-start(f16[128,2048]{1,0:T(8,128)(2,1)S(1)} %fusion.7), channel_id=1, source_target_pairs={{0,8},{8,0},{16,24},{24,16},{32,40},{40,32},{48,56},{56,48},{64,72... | collective-permute-start | bytes 1572872 | tf_op jit(solution)/shard_map/ppermute | solution.py:16
  213.6 21.7 %copy-start.4 = (s32[1024]{0:T(1024)S(1)}, s32[1024]{0:T(1024)}, u32[]{:S(2)}) copy-start(s32[1024]{0:T(1024)} %param.8) | copy-start | bytes 12292
  213.6 16.8 %collective-permute-start.8 = (bf16[128,2048]{1,0:T(8,128)(2,1)S(1)}, bf16[128,2048]{1,0:T(8,128)(2,1)S(1)}, u32[]{:S(2)}, u32[]{:S(2)}) collective-permute-start(bf16[128,2048]{1,0:T(8,128)(2,1)S(1)} %fusion.4), channel_id=1, source_target_pairs={{0,8},{8,0},{16,24},{24,16},{32,40},{40,32},{48,56},{56,48},{64,72... | collective-permute-start | bytes 1572872 | tf_op jit(solution)/shard_map/ppermute | solution.py:16
  221.1 14.6 %collective-permute-start.7 = (f32[4,128,250]{2,1,0:T(8,128)S(1)}, f32[4,128,250]{2,1,0:T(8,128)S(1)}, u32[]{:S(2)}, u32[]{:S(2)}) collective-permute-start(f32[4,128,250]{2,1,0:T(8,128)S(1)} %convolution_bitcast_fusion.1), channel_id=1, source_target_pairs={{0,4},{4,0},{1,5},{5,1},{2,6},{6,2},{3,7},{7,3},{8,12},{12,8},{9,1... | collective-permute-start | bytes 1536008 | tf_op jit(solution)/shard_map/ppermute | solution.py:40
  233.3 3.8 %collective-permute-start.9 = (f32[4,128,250]{2,1,0:T(8,128)S(1)}, f32[4,128,250]{2,1,0:T(8,128)S(1)}, u32[]{:S(2)}, u32[]{:S(2)}) collective-permute-start(f32[4,128,250]{2,1,0:T(8,128)S(1)} %convolution_bitcast_fusion), channel_id=1, source_target_pairs={{0,4},{4,0},{1,5},{5,1},{2,6},{6,2},{3,7},{7,3},{8,12},{12,8},{9,1... | collective-permute-start | bytes 1536008 | tf_op jit(solution)/shard_map/ppermute | solution.py:40
  238.6 35.0 %all-to-all-start.1 = ((f32[32,1,24]{2,1,0:T(1,128)}), f32[32,1,24]{2,1,0:T(1,128)S(1)}, u32[]{:S(2)}, u32[]{:S(2)}) async-start(f32[32,1,24]{2,1,0:T(1,128)} %bitcast.27), calls=%async_computation.1 | async-start | bytes 32768 | tf_op jit(solution)/shard_map/all_to_all | solution.py:139
where the time goes:
time: 275 us
  blocking collectives  150 us (55%)
  starting transfers between devices  50.2 us (18%)
  waiting for transfers between devices  47.5 us (17%)
  matrix products  11.7 us (4%)
  local copies, waits for them, and re-layouts  8.08 us (3%)
  other arithmetic  5.98 us (2%)
    all_gather x1, blocking collectives, device_step(): lax.all_gather(tokens, 'grid', axis=0, axis_index_groups=parity_groups(gr...  76.4 us
    psum x1, blocking collectives, device_step(): branch = lax.psum(pair_sum, 'grid', axis_index_groups=parity_groups(grid))  68.3 us
    ppermute x3, waiting for transfers between devices, swapped_in_pairs(): return lax.ppermute(value, axis, [(i, i ^ 1) for i in range(size)])  24.4 us
    all_to_all x1, waiting for transfers between devices, device_step(): lax.all_to_all(pieces, 'grid', 0, 0, tiled=True).reshape(grid, 3, own_rows)  21 us
    ppermute x4, starting transfers between devices, shifted(): lax.ppermute(value, axis, [(i, (i + step) % size) for i in range(size)])  13.9 us
    all_to_all x1, starting transfers between devices, device_step(): lax.all_to_all(pieces, 'grid', 0, 0, tiled=True).reshape(grid, 3, own_rows)  13.3 us
    ppermute x3, starting transfers between devices, swapped_in_pairs(): return lax.ppermute(value, axis, [(i, i ^ 1) for i in range(size)])  12.1 us
    ppermute x3, starting transfers between devices, both_halves(): return part + lax.ppermute(part, axis, [(0, 1), (1, 0)])  5.84 us
  transfers between devices with their start and end apart: 12, of which 6 were waited for; matrix products, arithmetic and copies ran while one was open for 7% of the time, Pallas kernels for 0%

commit v1 on v0

--- a/solution.py
+++ b/solution.py
@@ -120,11 +120,15 @@
         jnp.bfloat16
     )
     mixed = lax.dynamic_slice_in_dim(mixed_own, lax.div(lax.axis_index("grid"), 2) * own_rows, own_rows, 0)
-    held = lax.optimization_barrier(mixed_own).astype(jnp.float32)
-    squares = lax.psum(jnp.sum(held * held, axis=1), "row")
+    held = lax.optimization_barrier(mixed_own)
+    held_other = swapped_in_pairs(held, "grid")
+    squares = lax.psum(jnp.sum(jnp.square(held.astype(jnp.float32)), axis=1), "row")
     scale = lax.rsqrt(squares / features + 1e-05)
-    normed_own = (held * scale[:, None] * norm_gain[None, :]).astype(jnp.bfloat16)
-    normed_other = swapped_in_pairs(normed_own, "grid")
+    scale_other = swapped_in_pairs(scale, "grid")
+    normed_own, normed_other = (
+        (rows.astype(jnp.float32) * factor[:, None] * norm_gain[None, :]).astype(jnp.bfloat16)
+        for rows, factor in ((held, scale), (held_other, scale_other))
+    )
     targets = lax.dynamic_slice_in_dim(
         target_tokens.reshape(grid // 2, 2, rep, own_rows), lax.axis_index("rep"), 1, 2
     )[:, :, 0]

time: 275 us -> 270 us (0.982)
  the two profiles are of different devices: /device:TPU:40 before, /device:TPU:42 now
where the time goes in v1:
time: 270 us; the launch traced here: 269 us
  blocking collectives  150 us (56%)
  starting transfers between devices  53.9 us (20%)
  waiting for transfers between devices  38.7 us (14%)
  matrix products  11.8 us (4%)
  local copies, waits for them, and re-layouts  8.08 us (3%)
  other arithmetic  5.78 us (2%)
    all_gather x1, blocking collectives, device_step(): lax.all_gather(tokens, 'grid', axis=0, axis_index_groups=parity_groups(gr...  76.3 us
    psum x1, blocking collectives, device_step(): branch = lax.psum(pair_sum, 'grid', axis_index_groups=parity_groups(grid))  68.6 us
    all_to_all x1, waiting for transfers between devices, device_step(): lax.all_to_all(pieces, 'grid', 0, 0, tiled=True).reshape(grid, 3, own_rows)  21 us
    ppermute x4, waiting for transfers between devices, swapped_in_pairs(): return lax.ppermute(value, axis, [(i, i ^ 1) for i in range(size)])  16.5 us
    all_to_all x1, starting transfers between devices, device_step(): lax.all_to_all(pieces, 'grid', 0, 0, tiled=True).reshape(grid, 3, own_rows)  13.9 us
    ppermute x4, starting transfers between devices, swapped_in_pairs(): return lax.ppermute(value, axis, [(i, i ^ 1) for i in range(size)])  13.8 us
    ppermute x4, starting transfers between devices, shifted(): lax.ppermute(value, axis, [(i, (i + step) % size) for i in range(size)])  11.8 us
    all_to_all x1, starting transfers between devices, sent_to_all(): lax.all_to_all(jnp.broadcast_to(value[None], (peers, *value.shape)), axis...  8.07 us
  transfers between devices with their start and end apart: 13, of which 5 were waited for; matrix products, arithmetic and copies ran while one was open for 7% of the time, Pallas kernels for 0%

profile of v1, /device:TPU:42, one launch (start us, length us, event | category | flops | bytes accessed | tf_op | source)
XLA Modules:
  0.0 269.3 jit_solution(16684335265449489295)
XLA Ops:
  0.6 1.4 pad_maximum_fusion
  2.0 2.3 collective-permute-start
  4.4 3.6 %collective-permute-start.1 = (bf16[1344,512]{1,0:T(8,128)(2,1)S(1)}, bf16[1344,512]{1,0:T(8,128)(2,1)}, u32[]{:S(2)}, u32[]{:S(2)}) collective-permute-start(bf16[1344,512]{1,0:T(8,128)(2,1)S(1)} %pad_maximum_fusion), channel_id=1, source_target_pairs={{0,1},{1,2},{2,3},{3,0},{4,5},{5,6},{6,7},{7,4},{8,9},{9,10},{10,1... | collective-permute-start | bytes 4128776 | tf_op jit(solution)/shard_map/ppermute | solution.py:28
  8.0 76.3 %all-gather = bf16[128,2048]{1,0:T(8,128)(2,1)S(1)} all-gather(bf16[8,2048]{1,0:T(8,128)(2,1)} %param.7), channel_id=2, replica_groups={{0,16,32,48,64,80,96,112,128,144,160,176,192,208,224,240},{8,24,40,56,7..., dimensions={0}, use_global_device_ids=true | all-gather | bytes 557056 | tf_op jit(solution)/shard_map/all_gather | solution.py:93
  84.3 3.7 %collective-permute-start.3 = (bf16[672,512]{1,0:T(8,128)(2,1)S(1)}, bf16[672,512]{1,0:T(8,128)(2,1)S(1)}, u32[]{:S(2)}, u32[]{:S(2)}) collective-permute-start(bf16[672,512]{1,0:T(8,128)(2,1)S(1)} %slice.74), channel_id=1, source_target_pairs={{0,3},{1,0},{2,1},{3,2},{4,7},{5,4},{6,5},{7,6},{8,11},{9,8},{10,9... | collective-permute-start | bytes 2064392 | tf_op jit(solution)/shard_map/ppermute | solution.py:28
  87.9 1.1 slice.75
  89.1 2.2 collective-permute-start.4
  91.3 4.0 %collective-permute-start.2 = (bf16[128,2048]{1,0:T(8,128)(2,1)S(1)}, bf16[128,2048]{1,0:T(8,128)(2,1)S(1)}, u32[]{:S(2)}, u32[]{:S(2)}) collective-permute-start(bf16[128,2048]{1,0:T(8,128)(2,1)S(1)} %all-gather), channel_id=1, source_target_pairs={{0,8},{8,0},{16,24},{24,16},{32,40},{40,32},{48,56},{56,48},{64,72... | collective-permute-start | bytes 1572872 | tf_op jit(solution)/shard_map/ppermute | solution.py:16
  95.4 0.4 broadcast_in_dim.16
  95.8 0.1 bitcast_dynamic-update-slice_fusion.1
  95.9 1.5 bitcast_dynamic-update-slice_fusion
  97.4 5.1 %collective-permute-done.2 = bf16[128,2048]{1,0:T(8,128)(2,1)S(1)} collective-permute-done((bf16[128,2048]{1,0:T(8,128)(2,1)S(1)}, bf16[128,2048]{1,0:T(8,128)(2,1)S(1)}, u32[]{:S(2)}, u32[]{:S(2)}) %collective-permute-start.2) | collective-permute-done | bytes 524320 | tf_op jit(solution)/shard_map/ppermute | solution.py:16
  102.7 0.3 collective-permute-done.4
  103.0 0.5 fusion.10
  103.5 0.5 fusion.9
  104.0 0.5 fusion.8
  104.4 0.5 fusion.1
  104.9 0.5 copy-done
  105.4 1.9 collective-permute-start.5
  107.3 2.4 broadcast_in_dim.22
  109.7 8.1 %all-to-all-start = ((bf16[4,2048,250]{2,1,0:T(8,128)(2,1)}), bf16[4,2048,250]{2,1,0:T(8,128)(2,1)}, u32[]{:S(2)}, u32[]{:S(2)}) async-start(bf16[4,2048,250]{2,1,0:T(8,128)(2,1)} %broadcast_in_dim.22), calls=%async_computation | async-start | bytes 8388608 | tf_op jit(solution)/shard_map/all_to_all | solution.py:21
  117.8 0.3 abs_reduce_fusion
  118.1 2.5 psum.21
  120.6 1.4 add.96
  122.0 0.2 fusion.15
  122.3 1.5 fusion.22
  123.7 1.2 fusion.24
  125.0 0.2 fusion.26
  125.2 0.2 fusion.28
  125.5 0.2 fusion.7
  125.6 3.8 %collective-permute-start.6 = (f16[128,2048]{1,0:T(8,128)(2,1)S(1)}, f16[128,2048]{1,0:T(8,128)(2,1)S(1)}, u32[]{:S(2)}, u32[]{:S(2)}) collective-permute-start(f16[128,2048]{1,0:T(8,128)(2,1)S(1)} %fusion.7), channel_id=1, source_target_pairs={{0,8},{8,0},{16,24},{24,16},{32,40},{40,32},{48,56},{56,48},{64,72... | collective-permute-start | bytes 1572872 | tf_op jit(solution)/shard_map/ppermute | solution.py:16
  129.4 0.2 fusion.23
  129.6 0.2 fusion.25
  129.8 0.2 fusion.27
  130.1 0.2 fusion.29
  130.3 11.4 %collective-permute-done.6 = f16[128,2048]{1,0:T(8,128)(2,1)S(1)} collective-permute-done((f16[128,2048]{1,0:T(8,128)(2,1)S(1)}, f16[128,2048]{1,0:T(8,128)(2,1)S(1)}, u32[]{:S(2)}, u32[]{:S(2)}) %collective-permute-start.6) | collective-permute-done | bytes 524320 | tf_op jit(solution)/shard_map/ppermute | solution.py:16
  141.7 0.2 fusion.6
  141.9 68.6 %all-reduce.1 = u32[4,32768]{1,0:T(4,128)S(1)} all-reduce(u32[4,32768]{1,0:T(4,128)S(1)} %bitcast.79), channel_id=1, replica_groups={{0,16,32,48,64,80,96,112,128,144,160,176,192,208,224,240},{8,24,40,56,7..., use_global_device_ids=true, to_apply=%region_2.3.clone | all-reduce | flops 131072 | bytes 1048576 | tf_op jit(solution)/shard_map/psum | solution.py:118
  210.5 0.2 add_convert_fusion
  210.7 4.1 %collective-permute-start.8 = (bf16[128,2048]{1,0:T(8,128)(2,1)S(1)}, bf16[128,2048]{1,0:T(8,128)(2,1)S(1)}, u32[]{:S(2)}, u32[]{:S(2)}) collective-permute-start(bf16[128,2048]{1,0:T(8,128)(2,1)S(1)} %add_convert_fusion), channel_id=1, source_target_pairs={{0,8},{8,0},{16,24},{24,16},{32,40},{40,32},{48,56},{56,48},{64,72... | collective-permute-start | bytes 1572872 | tf_op jit(solution)/shard_map/ppermute | solution.py:16
  214.8 0.2 fusion.2
  215.0 2.5 psum.23
  217.5 1.9 collective-permute-start.9
  219.5 2.9 %convolution_bitcast_fusion.1 = f32[4,128,250]{2,1,0:T(8,128)S(1)} fusion(bf16[4,2048,250]{2,1,0:T(8,128)(2,1)} %all-to-all-done, bf16[128,2048]{1,0:T(8,128)(2,1)S(1)} %add_convert_fusion, f32[2048]{0:T(1024)S(1)} %copy-done.3, f32[128]{0:T(128)S(1)} %add_rsqrt_fusion), kind=kOutput, calls=%fused_computation.10 | convolution fusion | flops 525336576 | bytes 5140992 | tf_op jit(solution)/shard_map/tk,rkv->rtv/dot_general | solution.py:68
  222.4 2.1 collective-permute-start.7
  224.6 2.9 %convolution_bitcast_fusion = f32[4,128,250]{2,1,0:T(8,128)S(1)} fusion(bf16[4,2048,250]{2,1,0:T(8,128)(2,1)} %all-to-all-done, bf16[128,2048]{1,0:T(8,128)(2,1)S(1)} %collective-permute-done.8, f32[128]{0:T(128)S(1)} %collective-permute-done.9, f32[2048]{0:T(1024)S(1)} %copy-done.3), kind=kOutput, calls=%fused_computation.9 | convolution fusion | flops 525336576 | bytes 5140992 | tf_op jit(solution)/shard_map/tk,rkv->rtv/dot_general | solution.py:68
  227.5 2.3 collective-permute-start.10
  229.8 0.1 reshape.55
  230.0 0.1 subtract_reduce_fusion.1
  230.0 0.1 sub.61
  230.1 0.1 sub.66
  230.2 0.1 fusion.45
  230.4 1.0 collective-permute-done.10
  231.3 0.1 fusion.46
  231.5 0.4 exponential_reduce_fusion.1
  232.0 0.1 reshape.56
  232.1 0.7 all_to_all.10
  232.8 13.9 %all-to-all-start.1 = ((f32[32,1,24]{2,1,0:T(1,128)}), f32[32,1,24]{2,1,0:T(1,128)S(1)}, u32[]{:S(2)}, u32[]{:S(2)}) async-start(f32[32,1,24]{2,1,0:T(1,128)} %bitcast.27), calls=%async_computation.1 | async-start | bytes 32768 | tf_op jit(solution)/shard_map/all_to_all | solution.py:143
  246.7 0.6 constant_dynamic-slice_fusion
  247.3 21.0 %all-to-all-done.1 = f32[32,1,24]{2,1,0:T(1,128)S(1)} async-done(((f32[32,1,24]{2,1,0:T(1,128)}), f32[32,1,24]{2,1,0:T(1,128)S(1)}, u32[]{:S(2)}, u32[]{:S(2)}) %all-to-all-start.1) | async-done | bytes 3104 | tf_op jit(solution)/shard_map/all_to_all | solution.py:143
  268.3 0.1 copy.16
  268.4 0.2 slice_reduce_fusion
  268.5 0.2 fusion.43
  268.7 0.5 log_subtract_fusion
  (32 shorter events, 0.4 us)
Async XLA Ops:
  2.0 82.2 %collective-permute-start = (bf16[1344,512]{1,0:T(8,128)(2,1)S(1)}, bf16[1344,512]{1,0:T(8,128)(2,1)S(1)}, u32[]{:S(2)}, u32[]{:S(2)}) collective-permute-start(bf16[1344,512]{1,0:T(8,128)(2,1)S(1)} %pad_maximum_fusion), channel_id=1, source_target_pairs={{0,3},{1,0},{2,1},{3,2},{4,7},{5,4},{6,5},{7,6},{8,11},{9,8},{10,9... | collective-permute-start | bytes 4128776 | tf_op jit(solution)/shard_map/ppermute | solution.py:28
  4.4 79.9 %collective-permute-start.1 = (bf16[1344,512]{1,0:T(8,128)(2,1)S(1)}, bf16[1344,512]{1,0:T(8,128)(2,1)}, u32[]{:S(2)}, u32[]{:S(2)}) collective-permute-start(bf16[1344,512]{1,0:T(8,128)(2,1)S(1)} %pad_maximum_fusion), channel_id=1, source_target_pairs={{0,1},{1,2},{2,3},{3,0},{4,5},{5,6},{6,7},{7,4},{8,9},{9,10},{10,1... | collective-permute-start | bytes 4128776 | tf_op jit(solution)/shard_map/ppermute | solution.py:28
  84.3 18.3 %collective-permute-start.3 = (bf16[672,512]{1,0:T(8,128)(2,1)S(1)}, bf16[672,512]{1,0:T(8,128)(2,1)S(1)}, u32[]{:S(2)}, u32[]{:S(2)}) collective-permute-start(bf16[672,512]{1,0:T(8,128)(2,1)S(1)} %slice.74), channel_id=1, source_target_pairs={{0,3},{1,0},{2,1},{3,2},{4,7},{5,4},{6,5},{7,6},{8,11},{9,8},{10,9... | collective-permute-start | bytes 2064392 | tf_op jit(solution)/shard_map/ppermute | solution.py:28
  89.1 13.8 %collective-permute-start.4 = (bf16[672,512]{1,0:T(8,128)(2,1)S(1)}, bf16[672,512]{1,0:T(8,128)(2,1)S(1)}, u32[]{:S(2)}, u32[]{:S(2)}) collective-permute-start(bf16[672,512]{1,0:T(8,128)(2,1)S(1)} %slice.75), channel_id=1, source_target_pairs={{0,1},{1,2},{2,3},{3,0},{4,5},{5,6},{6,7},{7,4},{8,9},{9,10},{10,1... | collective-permute-start | bytes 2064392 | tf_op jit(solution)/shard_map/ppermute | solution.py:28
  91.3 11.2 %collective-permute-start.2 = (bf16[128,2048]{1,0:T(8,128)(2,1)S(1)}, bf16[128,2048]{1,0:T(8,128)(2,1)S(1)}, u32[]{:S(2)}, u32[]{:S(2)}) collective-permute-start(bf16[128,2048]{1,0:T(8,128)(2,1)S(1)} %all-gather), channel_id=1, source_target_pairs={{0,8},{8,0},{16,24},{24,16},{32,40},{40,32},{48,56},{56,48},{64,72... | collective-permute-start | bytes 1572872 | tf_op jit(solution)/shard_map/ppermute | solution.py:16
  103.0 2.4 copy-start
  103.0 4.3 %copy-start.2 = (bf16[2048,250]{1,0:T(8,128)(2,1)S(1)}, bf16[2048,250]{1,0:T(8,128)(2,1)}, u32[]{:S(2)}) copy-start(bf16[2048,250]{1,0:T(8,128)(2,1)} %param.13) | copy-start | bytes 3072004
  105.4 15.2 %collective-permute-start.5 = (f32[256,896]{1,0:T(8,128)S(1)}, f32[256,896]{1,0:T(8,128)}, u32[]{:S(2)}, u32[]{:S(2)}) collective-permute-start(f32[256,896]{1,0:T(8,128)S(1)} %fusion.1), channel_id=1, source_target_pairs={{0,4},{4,0},{1,5},{5,1},{2,6},{6,2},{3,7},{7,3},{8,12},{12,8},{9,1... | collective-permute-start | bytes 2752520 | tf_op jit(solution)/shard_map/ppermute | solution.py:40
  109.7 109.8 %all-to-all-start = ((bf16[4,2048,250]{2,1,0:T(8,128)(2,1)}), bf16[4,2048,250]{2,1,0:T(8,128)(2,1)}, u32[]{:S(2)}, u32[]{:S(2)}) async-start(bf16[4,2048,250]{2,1,0:T(8,128)(2,1)} %broadcast_in_dim.22), calls=%async_computation | async-start | bytes 8388608 | tf_op jit(solution)/shard_map/all_to_all | solution.py:21
  120.6 4.4 %copy-start.1 = (bf16[4,1344,512]{2,1,0:T(8,128)(2,1)S(1)}, bf16[4,1344,512]{2,1,0:T(8,128)(2,1)}, u32[]{:S(2)}) copy-start(bf16[4,1344,512]{2,1,0:T(8,128)(2,1)} %copy-done) | copy-start | bytes 16515076
  125.2 94.3 %copy-start.3 = (f32[2048]{0:T(1024)S(1)}, f32[2048]{0:T(1024)}, u32[]{:S(2)}) copy-start(f32[2048]{0:T(1024)} %param.12) | copy-start | bytes 24580
  125.6 16.1 %collective-permute-start.6 = (f16[128,2048]{1,0:T(8,128)(2,1)S(1)}, f16[128,2048]{1,0:T(8,128)(2,1)S(1)}, u32[]{:S(2)}, u32[]{:S(2)}) collective-permute-start(f16[128,2048]{1,0:T(8,128)(2,1)S(1)} %fusion.7), channel_id=1, source_target_pairs={{0,8},{8,0},{16,24},{24,16},{32,40},{40,32},{48,56},{56,48},{64,72... | collective-permute-start | bytes 1572872 | tf_op jit(solution)/shard_map/ppermute | solution.py:16
  210.7 19.1 %copy-start.4 = (s32[1024]{0:T(1024)S(1)}, s32[1024]{0:T(1024)}, u32[]{:S(2)}) copy-start(s32[1024]{0:T(1024)} %param.8) | copy-start | bytes 12292
  210.7 13.8 %collective-permute-start.8 = (bf16[128,2048]{1,0:T(8,128)(2,1)S(1)}, bf16[128,2048]{1,0:T(8,128)(2,1)S(1)}, u32[]{:S(2)}, u32[]{:S(2)}) collective-permute-start(bf16[128,2048]{1,0:T(8,128)(2,1)S(1)} %add_convert_fusion), channel_id=1, source_target_pairs={{0,8},{8,0},{16,24},{24,16},{32,40},{40,32},{48,56},{56,48},{64,72... | collective-permute-start | bytes 1572872 | tf_op jit(solution)/shard_map/ppermute | solution.py:16
  217.5 7.0 %collective-permute-start.9 = (f32[128]{0:T(128)S(1)}, f32[128]{0:T(128)S(1)}, u32[]{:S(2)}, u32[]{:S(2)}) collective-permute-start(f32[128]{0:T(128)S(1)} %add_rsqrt_fusion), channel_id=1, source_target_pairs={{0,8},{8,0},{16,24},{24,16},{32,40},{40,32},{48,56},{56,48},{64,72... | collective-permute-start | bytes 1544 | tf_op jit(solution)/shard_map/ppermute | solution.py:16
  222.4 7.8 %collective-permute-start.7 = (f32[4,128,250]{2,1,0:T(8,128)S(1)}, f32[4,128,250]{2,1,0:T(8,128)S(1)}, u32[]{:S(2)}, u32[]{:S(2)}) collective-permute-start(f32[4,128,250]{2,1,0:T(8,128)S(1)} %convolution_bitcast_fusion.1), channel_id=1, source_target_pairs={{0,4},{4,0},{1,5},{5,1},{2,6},{6,2},{3,7},{7,3},{8,12},{12,8},{9,1... | collective-permute-start | bytes 1536008 | tf_op jit(solution)/shard_map/ppermute | solution.py:40
  227.5 3.8 %collective-permute-start.10 = (f32[4,128,250]{2,1,0:T(8,128)S(1)}, f32[4,128,250]{2,1,0:T(8,128)S(1)}, u32[]{:S(2)}, u32[]{:S(2)}) collective-permute-start(f32[4,128,250]{2,1,0:T(8,128)S(1)} %convolution_bitcast_fusion), channel_id=1, source_target_pairs={{0,4},{4,0},{1,5},{5,1},{2,6},{6,2},{3,7},{7,3},{8,12},{12,8},{9,1... | collective-permute-start | bytes 1536008 | tf_op jit(solution)/shard_map/ppermute | solution.py:40
  232.8 35.5 %all-to-all-start.1 = ((f32[32,1,24]{2,1,0:T(1,128)}), f32[32,1,24]{2,1,0:T(1,128)S(1)}, u32[]{:S(2)}, u32[]{:S(2)}) async-start(f32[32,1,24]{2,1,0:T(1,128)} %bitcast.27), calls=%async_computation.1 | async-start | bytes 32768 | tf_op jit(solution)/shard_map/all_to_all | solution.py:143

commit v2 on v1

--- a/solution.py
+++ b/solution.py
@@ -28,40 +28,23 @@
     return lax.ppermute(value, axis, [(i, (i + step) % size) for i in range(size)])
 
 
-def placed(parts, axis, size):
-    out = jnp.broadcast_to(parts[0][None], (size, *parts[0].shape))
-    for step, value, first_row in parts[1:]:
-        place = lax.rem(lax.axis_index(axis) + (step + size), size)
-        out = lax.dynamic_update_slice(out, value[None], (place, first_row, 0))
-    return out
+def turned(blocks, axis, sign):
+    size = len(blocks)
+    place = lax.axis_index(axis)
+    return [
+        lax.select_n(place, *(blocks[(k + sign * j) % size] for j in range(size))) for k in range(size)
+    ]
 
 
 def both_halves(part, axis):
     return part + lax.ppermute(part, axis, [(0, 1), (1, 0)])
 
 
-def hidden_units(rows, blocks, width):
-    features = blocks.shape[2]
-    part = sum(
-        lax.dot_general(
-            rows[:, k * features : (k + 1) * features],
-            blocks[k, :width],
-            (((1,), (1,)), ((), ())),
-            preferred_element_type=jnp.float32,
-        )
-        for k in range(blocks.shape[0])
+def summed_products(parts, weights):
+    return sum(
+        lax.dot_general(p, w, (((1,), (1,)), ((), ())), preferred_element_type=jnp.float32)
+        for p, w in zip(parts, weights)
     )
-    value = both_halves(part, "row")
-    gate_value, up_value = jnp.split(value, 2, axis=1)
-    return (jax.nn.silu(gate_value) * up_value).astype(jnp.bfloat16)
-
-
-def projected(hidden, blocks, width):
-    out = [
-        jnp.dot(hidden, blocks[k, width:], preferred_element_type=jnp.float32)
-        for k in range(blocks.shape[0])
-    ]
-    return jnp.concatenate(out, axis=1)
 
 
 def row_stats(normed, weights, targets, column_start):
@@ -85,35 +68,48 @@
     rep = lax.axis_size("rep")
     side = lax.rem(lax.axis_index("grid"), 2)
 
-    block = jnp.concatenate([gate_weight.T, up_weight.T, down_weight], axis=0)
+    units = down_weight.shape[0]
+    block = jnp.concatenate([gate_weight.T, down_weight, up_weight.T], axis=0)
     after = shifted(block, "rep", -1)
     before = shifted(block, "rep", 1)
-    width = gate_weight.shape[1] + up_weight.shape[1]
 
     own = lax.all_gather(tokens, "grid", axis=0, axis_index_groups=parity_groups(grid))
     own = own.reshape(-1, half_width)
-    own, after_held, before_held = lax.optimization_barrier((own, after, before))
+    own, after, before = lax.optimization_barrier((own, after, before))
     middle = block.shape[0] // 2
-    far_first = shifted(after_held[:middle], "rep", -1)
-    far_last = shifted(before_held[middle:], "rep", 1)
+    far_first = shifted(after[:middle], "rep", -1)
+    far_last = shifted(before[middle:], "rep", 1)
     other = swapped_in_pairs(own, "grid")
     vocab = sent_to_all(vocab_weight, "rep")
-    blocks = placed(
-        [block, (1, after_held, 0), (-1, before_held, 0), (2, far_first, 0), (2, far_last, middle)],
-        "rep",
-        rep,
-    )
-    rows = jnp.concatenate([other, own], axis=0)
-    length = lax.psum(jnp.sum(jnp.abs(rows.astype(jnp.float32)), axis=1), "row")
-    units = down_weight.shape[0] * grid
-    reach = jnp.maximum(jnp.square(GATE_UP_REACH * length) * (DOWN_REACH * units), 1e-20) / 30000.0
+    parts = [
+        jnp.concatenate(pair, axis=0)
+        for pair in zip(
+            turned(jnp.split(other, rep, axis=1), "rep", 1), turned(jnp.split(own, rep, axis=1), "rep", 1)
+        )
+    ]
+    length = lax.psum(sum(jnp.sum(jnp.abs(p.astype(jnp.float32)), axis=1) for p in parts), "row")
+    reach = jnp.square(GATE_UP_REACH * length) * (DOWN_REACH * units * grid)
+    reach = jnp.maximum(reach, 1e-20) / 30000.0
     share = (1.0 / reach)[:, None]
     half = own.shape[0]
 
-    hidden = hidden_units(rows, blocks, width)
-    branch_other = (projected(hidden[:half], blocks, width) * share[:half]).astype(jnp.float16)
-    arrived = swapped_in_pairs(branch_other, "grid")
-    branch_own = projected(hidden[half:], blocks, width) * share[half:]
+    gate_part = summed_products(
+        parts, [block[:units], after[:units], far_first[:units], before[:units]]
+    )
+    up_part = summed_products(
+        parts,
+        [block[2 * units :], after[2 * units :], far_last[2 * units - middle :], before[2 * units :]],
+    )
+    gate_value, up_value = both_halves(gate_part, "row"), both_halves(up_part, "row")
+    hidden = (jax.nn.silu(gate_value) * up_value).astype(jnp.bfloat16)
+    far_down = jnp.concatenate([far_first[units:], far_last[: 2 * units - middle]], axis=0)
+    downs = [block[units : 2 * units], after[units : 2 * units], far_down, before[units : 2 * units]]
+    branch = [jnp.dot(hidden, w, preferred_element_type=jnp.float32) for w in downs]
+    branch_other, branch_own = (
+        jnp.concatenate(turned([p[side] for p in branch], "rep", -1), axis=1) * share[side]
+        for side in (slice(0, half), slice(half, 2 * half))
+    )
+    arrived = swapped_in_pairs(branch_other.astype(jnp.float16), "grid")
     pair_sum = (branch_own + arrived.astype(jnp.float32)).astype(jnp.float16)
     branch = lax.psum(pair_sum, "grid", axis_index_groups=parity_groups(grid))
     mixed_own = (own.astype(jnp.float32) + branch.astype(jnp.float32) * reach[half:, None]).astype(
@@ -158,6 +154,4 @@
         P("row", ("grid", "rep")),
     )
     out_specs = (P(("groups", "grid", "rep"), "row"), P(("groups", "grid", "rep")))
-    return jax.shard_map(
-        device_step, mesh=mesh, in_specs=in_specs, out_specs=out_specs, check_vma=False
-    )
+    return jax.shard_map(device_step, mesh=mesh, in_specs=in_specs, out_specs=out_specs, check_vma=False)

time: 270 us -> 313 us (1.16)
  the two profiles are of different devices: /device:TPU:42 before, /device:TPU:33 now
where the time goes in v2:
time: 313 us; the launch traced here: 312 us
  blocking collectives  149 us (48%)
  waiting for transfers between devices  74.8 us (24%)
  starting transfers between devices  62.7 us (20%)
  matrix products  10.7 us (3%)
  local copies, waits for them, and re-layouts  7.5 us (2%)
  other arithmetic  6.12 us (2%)
    all_gather x1, blocking collectives, device_step(): lax.all_gather(tokens, 'grid', axis=0, axis_index_groups=parity_groups(gr...  69.2 us
    psum x1, blocking collectives, device_step(): branch = lax.psum(pair_sum, 'grid', axis_index_groups=parity_groups(grid))  60 us
    ppermute x4, waiting for transfers between devices, shifted(): lax.ppermute(value, axis, [(i, (i + step) % size) for i in range(size)])  40.5 us
    ppermute x4, starting transfers between devices, both_halves(): return part + lax.ppermute(part, axis, [(0, 1), (1, 0)])  20.7 us
    all_to_all x1, waiting for transfers between devices, device_step(): lax.all_to_all(pieces, 'grid', 0, 0, tiled=True).reshape(grid, 3, own_rows)  20 us
    psum x1, blocking collectives, device_step(): lax.psum(jnp.sum(jnp.square(held.astype(jnp.float32)), axis=1), 'row')  17.3 us
    ppermute x4, starting transfers between devices, shifted(): lax.ppermute(value, axis, [(i, (i + step) % size) for i in range(size)])  14.6 us
    ppermute x4, waiting for transfers between devices, swapped_in_pairs(): return lax.ppermute(value, axis, [(i, i ^ 1) for i in range(size)])  13.1 us
  transfers between devices with their start and end apart: 14, of which 4 were waited for; matrix products, arithmetic and copies ran while one was open for 6% of the time, Pallas kernels for 0%

profile of v2, /device:TPU:33, one launch (start us, length us, event | category | flops | bytes accessed | tf_op | source)
XLA Modules:
  0.0 312.2 jit_solution(15082182827361347012)
XLA Ops:
  0.6 1.5 pad_maximum_fusion
  2.1 5.6 %collective-permute-start = (bf16[1344,512]{1,0:T(8,128)(2,1)S(1)}, bf16[1344,512]{1,0:T(8,128)(2,1)S(1)}, u32[]{:S(2)}, u32[]{:S(2)}) collective-permute-start(bf16[1344,512]{1,0:T(8,128)(2,1)S(1)} %pad_maximum_fusion), channel_id=1, source_target_pairs={{0,3},{1,0},{2,1},{3,2},{4,7},{5,4},{6,5},{7,6},{8,11},{9,8},{10,9... | collective-permute-start | bytes 4128776 | tf_op jit(solution)/shard_map/ppermute | solution.py:28
  7.8 2.0 collective-permute-start.1
  9.7 69.2 %all-gather = bf16[128,2048]{1,0:T(8,128)(2,1)S(1)} all-gather(bf16[8,2048]{1,0:T(8,128)(2,1)S(1)} %copy-done.9), channel_id=2, replica_groups={{0,16,32,48,64,80,96,112,128,144,160,176,192,208,224,240},{8,24,40,56,7..., dimensions={0}, use_global_device_ids=true | all-gather | bytes 557056 | tf_op jit(solution)/shard_map/all_gather | solution.py:76
  78.9 1.2 copy-done.4
  80.1 3.5 %collective-permute-start.2 = (bf16[128,2048]{1,0:T(8,128)(2,1)S(1)}, bf16[128,2048]{1,0:T(8,128)(2,1)S(1)}, u32[]{:S(2)}, u32[]{:S(2)}) collective-permute-start(bf16[128,2048]{1,0:T(8,128)(2,1)S(1)} %all-gather), channel_id=1, source_target_pairs={{0,8},{8,0},{16,24},{24,16},{32,40},{40,32},{48,56},{56,48},{64,72... | collective-permute-start | bytes 1572872 | tf_op jit(solution)/shard_map/ppermute | solution.py:16
  83.6 2.2 broadcast_in_dim.6
  85.9 4.9 %all-to-all-start = ((bf16[4,2048,250]{2,1,0:T(8,128)(2,1)}), bf16[4,2048,250]{2,1,0:T(8,128)(2,1)}, u32[]{:S(2)}, u32[]{:S(2)}) async-start(bf16[4,2048,250]{2,1,0:T(8,128)(2,1)} %broadcast_in_dim.6), calls=%async_computation | async-start | bytes 8388608 | tf_op jit(solution)/shard_map/all_to_all | solution.py:21
  90.9 1.1 slice.86
  92.0 3.3 %collective-permute-start.5 = (bf16[672,512]{1,0:T(8,128)(2,1)S(1)}, bf16[672,512]{1,0:T(8,128)(2,1)S(1)}, u32[]{:S(2)}, u32[]{:S(2)}) collective-permute-start(bf16[672,512]{1,0:T(8,128)(2,1)S(1)} %slice.86), channel_id=1, source_target_pairs={{0,1},{1,2},{2,3},{3,0},{4,5},{5,6},{6,7},{7,4},{8,9},{9,10},{10,1... | collective-permute-start | bytes 2064392 | tf_op jit(solution)/shard_map/ppermute | solution.py:28
  95.3 3.8 %collective-permute-start.3 = (bf16[672,512]{1,0:T(8,128)(2,1)S(1)}, bf16[672,512]{1,0:T(8,128)(2,1)S(1)}, u32[]{:S(2)}, u32[]{:S(2)}) collective-permute-start(bf16[672,512]{1,0:T(8,128)(2,1)S(1)} %slice.82), channel_id=1, source_target_pairs={{0,3},{1,0},{2,1},{3,2},{4,7},{5,4},{6,5},{7,6},{8,11},{9,8},{10,9... | collective-permute-start | bytes 2064392 | tf_op jit(solution)/shard_map/ppermute | solution.py:28
  99.3 0.3 fusion.34
  99.6 0.2 abs_reduce_fusion.2
  99.8 0.3 convolution_add_fusion.1
  100.1 0.8 copy-done.5
  100.9 0.3 fusion.28
  101.2 0.2 abs_reduce_fusion
  101.4 0.3 fusion.31
  101.7 0.2 copy-done.1
  102.0 0.3 fusion.35
  102.3 0.3 convolution_add_fusion.3
  102.6 40.5 %collective-permute-done.5 = bf16[672,512]{1,0:T(8,128)(2,1)S(1)} collective-permute-done((bf16[672,512]{1,0:T(8,128)(2,1)S(1)}, bf16[672,512]{1,0:T(8,128)(2,1)S(1)}, u32[]{:S(2)}, u32[]{:S(2)}) %collective-permute-start.5) | collective-permute-done | bytes 688160 | tf_op jit(solution)/shard_map/ppermute | solution.py:28
  143.1 0.3 fusion
  143.4 14.2 %collective-permute-start.6 = (f32[256,448]{0,1:T(8,128)S(1)}, f32[256,448]{0,1:T(8,128)S(1)}, u32[]{:S(2)}, u32[]{:S(2)}) collective-permute-start(f32[256,448]{0,1:T(8,128)S(1)} %fusion), channel_id=1, source_target_pairs={{0,4},{4,0},{1,5},{5,1},{2,6},{6,2},{3,7},{7,3},{8,12},{12,8},{9,1... | collective-permute-start | bytes 1376264 | tf_op jit(solution)/shard_map/ppermute | solution.py:40
  157.6 0.3 fusion.1
  157.9 2.0 collective-permute-start.4
  159.9 2.7 psum.21
  162.6 1.2 multiply_convert_fusion.1
  163.8 0.3 fusion.24
  164.2 1.4 fusion.26
  165.6 0.3 fusion.51
  165.9 0.3 fusion.20
  166.2 0.2 select_select_fusion.3
  166.5 0.2 select_select_fusion.2
  166.7 0.2 fusion.7
  166.9 2.0 collective-permute-start.7
  168.9 13.1 %collective-permute-done.7 = f16[128,2048]{1,0:T(8,128)(2,1)S(1)} collective-permute-done((f16[128,2048]{1,0:T(8,128)(2,1)S(1)}, f16[128,2048]{1,0:T(8,128)(2,1)S(1)}, u32[]{:S(2)}, u32[]{:S(2)}) %collective-permute-start.7) | collective-permute-done | bytes 524320 | tf_op jit(solution)/shard_map/ppermute | solution.py:16
  182.0 0.2 fusion.6
  182.2 60.0 %all-reduce.1 = u32[4,32768]{1,0:T(4,128)S(1)} all-reduce(u32[4,32768]{1,0:T(4,128)S(1)} %bitcast.50), channel_id=1, replica_groups={{0,16,32,48,64,80,96,112,128,144,160,176,192,208,224,240},{8,24,40,56,7..., use_global_device_ids=true, to_apply=%region_5.6.clone | all-reduce | flops 131072 | bytes 1048576 | tf_op jit(solution)/shard_map/psum | solution.py:114
  242.2 0.2 add_convert_fusion
  242.4 2.0 collective-permute-start.9
  244.4 0.2 fusion.2
  244.6 17.3 %psum.23 = f32[128]{0:T(128)S(1)} all-reduce(f32[128]{0:T(128)S(1)} %fusion.2), channel_id=1, replica_groups=mesh['groups'=2,'grid'=32,'row'=2,'rep'=4] {'row'}, use_global_device_ids=true, to_apply=%region_7.8 | all-reduce | flops 128 | bytes 1024 | tf_op jit(solution)/shard_map/psum | solution.py:121
  261.9 3.3 %collective-permute-start.10 = (f32[128]{0:T(128)S(1)}, f32[128]{0:T(128)S(1)}, u32[]{:S(2)}, u32[]{:S(2)}) collective-permute-start(f32[128]{0:T(128)S(1)} %add_rsqrt_fusion), channel_id=1, source_target_pairs={{0,8},{8,0},{16,24},{24,16},{32,40},{40,32},{48,56},{56,48},{64,72... | collective-permute-start | bytes 1544 | tf_op jit(solution)/shard_map/ppermute | solution.py:16
  265.1 2.9 convolution_bitcast_fusion.1
  268.1 2.6 collective-permute-start.8
  270.7 2.9 convolution_bitcast_fusion
  273.7 2.0 collective-permute-start.11
  275.6 0.1 reshape.54
  275.9 0.1 sub.61
  276.0 0.1 sub.66
  276.1 0.1 fusion.48
  276.2 1.3 collective-permute-done.11
  277.5 0.1 fusion.49
  277.6 0.4 exponential_reduce_fusion.1
  278.1 0.1 reshape.55
  278.3 0.7 all_to_all.10
  278.9 11.7 %all-to-all-start.1 = ((f32[32,1,24]{2,1,0:T(1,128)}), f32[32,1,24]{2,1,0:T(1,128)S(1)}, u32[]{:S(2)}, u32[]{:S(2)}) async-start(f32[32,1,24]{2,1,0:T(1,128)} %bitcast.15), calls=%async_computation.1 | async-start | bytes 32768 | tf_op jit(solution)/shard_map/all_to_all | solution.py:139
  290.7 0.6 constant_dynamic-slice_fusion
  291.3 20.0 %all-to-all-done.1 = f32[32,1,24]{2,1,0:T(1,128)S(1)} async-done(((f32[32,1,24]{2,1,0:T(1,128)}), f32[32,1,24]{2,1,0:T(1,128)S(1)}, u32[]{:S(2)}, u32[]{:S(2)}) %all-to-all-start.1) | async-done | bytes 3104 | tf_op jit(solution)/shard_map/all_to_all | solution.py:139
  311.3 0.1 copy.16
  311.4 0.2 slice_reduce_fusion
  311.5 0.2 fusion.37
  311.7 0.5 log_subtract_fusion
  (49 shorter events, 0.4 us)
Async XLA Ops:
  0.6 9.1 %copy-start.9 = (bf16[8,2048]{1,0:T(8,128)(2,1)S(1)}, bf16[8,2048]{1,0:T(8,128)(2,1)}, u32[]{:S(2)}) copy-start(bf16[8,2048]{1,0:T(8,128)(2,1)} %param.7) | copy-start | bytes 98308
  0.6 83.0 %copy-start.3 = (bf16[2048,250]{1,0:T(8,128)(2,1)S(1)}, bf16[2048,250]{1,0:T(8,128)(2,1)}, u32[]{:S(2)}) copy-start(bf16[2048,250]{1,0:T(8,128)(2,1)} %param.13) | copy-start | bytes 3072004
  2.1 76.8 %collective-permute-start = (bf16[1344,512]{1,0:T(8,128)(2,1)S(1)}, bf16[1344,512]{1,0:T(8,128)(2,1)S(1)}, u32[]{:S(2)}, u32[]{:S(2)}) collective-permute-start(bf16[1344,512]{1,0:T(8,128)(2,1)S(1)} %pad_maximum_fusion), channel_id=1, source_target_pairs={{0,3},{1,0},{2,1},{3,2},{4,7},{5,4},{6,5},{7,6},{8,11},{9,8},{10,9... | collective-permute-start | bytes 4128776 | tf_op jit(solution)/shard_map/ppermute | solution.py:28
  7.8 71.1 %collective-permute-start.1 = (bf16[1344,512]{1,0:T(8,128)(2,1)S(1)}, bf16[1344,512]{1,0:T(8,128)(2,1)S(1)}, u32[]{:S(2)}, u32[]{:S(2)}) collective-permute-start(bf16[1344,512]{1,0:T(8,128)(2,1)S(1)} %pad_maximum_fusion), channel_id=1, source_target_pairs={{0,1},{1,2},{2,3},{3,0},{4,5},{5,6},{6,7},{7,4},{8,9},{9,10},{10,1... | collective-permute-start | bytes 4128776 | tf_op jit(solution)/shard_map/ppermute | solution.py:28
  78.9 1.2 copy-start.4
  80.1 19.1 %collective-permute-start.2 = (bf16[128,2048]{1,0:T(8,128)(2,1)S(1)}, bf16[128,2048]{1,0:T(8,128)(2,1)S(1)}, u32[]{:S(2)}, u32[]{:S(2)}) collective-permute-start(bf16[128,2048]{1,0:T(8,128)(2,1)S(1)} %all-gather), channel_id=1, source_target_pairs={{0,8},{8,0},{16,24},{24,16},{32,40},{40,32},{48,56},{56,48},{64,72... | collective-permute-start | bytes 1572872 | tf_op jit(solution)/shard_map/ppermute | solution.py:16
  85.9 179.2 %all-to-all-start = ((bf16[4,2048,250]{2,1,0:T(8,128)(2,1)}), bf16[4,2048,250]{2,1,0:T(8,128)(2,1)}, u32[]{:S(2)}, u32[]{:S(2)}) async-start(bf16[4,2048,250]{2,1,0:T(8,128)(2,1)} %broadcast_in_dim.6), calls=%async_computation | async-start | bytes 8388608 | tf_op jit(solution)/shard_map/all_to_all | solution.py:21
  92.0 51.0 %collective-permute-start.5 = (bf16[672,512]{1,0:T(8,128)(2,1)S(1)}, bf16[672,512]{1,0:T(8,128)(2,1)S(1)}, u32[]{:S(2)}, u32[]{:S(2)}) collective-permute-start(bf16[672,512]{1,0:T(8,128)(2,1)S(1)} %slice.86), channel_id=1, source_target_pairs={{0,1},{1,2},{2,3},{3,0},{4,5},{5,6},{6,7},{7,4},{8,9},{9,10},{10,1... | collective-permute-start | bytes 2064392 | tf_op jit(solution)/shard_map/ppermute | solution.py:28
  95.3 3.9 %copy-start = (bf16[512,448]{0,1:T(8,128)(2,1)S(1)}, bf16[512,448]{0,1:T(8,128)(2,1)}, u32[]{:S(2)}) copy-start(bf16[512,448]{0,1:T(8,128)(2,1)} %param.10) | copy-start | bytes 1376260
  95.3 62.2 %collective-permute-start.3 = (bf16[672,512]{1,0:T(8,128)(2,1)S(1)}, bf16[672,512]{1,0:T(8,128)(2,1)S(1)}, u32[]{:S(2)}, u32[]{:S(2)}) collective-permute-start(bf16[672,512]{1,0:T(8,128)(2,1)S(1)} %slice.82), channel_id=1, source_target_pairs={{0,3},{1,0},{2,1},{3,2},{4,7},{5,4},{6,5},{7,6},{8,11},{9,8},{10,9... | collective-permute-start | bytes 2064392 | tf_op jit(solution)/shard_map/ppermute | solution.py:28
  99.6 1.3 copy-start.5
  100.9 1.0 copy-start.1
  143.0 14.9 %copy-start.6 = (bf16[672,512]{1,0:T(8,128)(2,1)}, bf16[672,512]{1,0:T(8,128)(2,1)S(1)}, u32[]{:S(2)}) copy-start(bf16[672,512]{1,0:T(8,128)(2,1)S(1)} %collective-permute-done.5) | copy-start | bytes 2064388
  143.4 19.3 %collective-permute-start.6 = (f32[256,448]{0,1:T(8,128)S(1)}, f32[256,448]{0,1:T(8,128)S(1)}, u32[]{:S(2)}, u32[]{:S(2)}) collective-permute-start(f32[256,448]{0,1:T(8,128)S(1)} %fusion), channel_id=1, source_target_pairs={{0,4},{4,0},{1,5},{5,1},{2,6},{6,2},{3,7},{7,3},{8,12},{12,8},{9,1... | collective-permute-start | bytes 1376264 | tf_op jit(solution)/shard_map/ppermute | solution.py:40
  157.6 2.3 copy-start.7
  157.9 4.7 %collective-permute-start.4 = (f32[256,448]{0,1:T(8,128)S(1)}, f32[256,448]{0,1:T(8,128)}, u32[]{:S(2)}, u32[]{:S(2)}) collective-permute-start(f32[256,448]{0,1:T(8,128)S(1)} %fusion.1), channel_id=1, source_target_pairs={{0,4},{4,0},{1,5},{5,1},{2,6},{6,2},{3,7},{7,3},{8,12},{12,8},{9,1... | collective-permute-start | bytes 1376264 | tf_op jit(solution)/shard_map/ppermute | solution.py:40
  163.8 1.8 copy-start.2
  164.1 1.8 slice-start
  164.1 1.8 slice-start.1
  166.9 15.1 %collective-permute-start.7 = (f16[128,2048]{1,0:T(8,128)(2,1)S(1)}, f16[128,2048]{1,0:T(8,128)(2,1)S(1)}, u32[]{:S(2)}, u32[]{:S(2)}) collective-permute-start(f16[128,2048]{1,0:T(8,128)(2,1)S(1)} %fusion.7), channel_id=1, source_target_pairs={{0,8},{8,0},{16,24},{24,16},{32,40},{40,32},{48,56},{56,48},{64,72... | collective-permute-start | bytes 1572872 | tf_op jit(solution)/shard_map/ppermute | solution.py:16
  182.2 82.9 %copy-start.8 = (f32[2048]{0:T(1024)S(1)}, f32[2048]{0:T(1024)}, u32[]{:S(2)}) copy-start(f32[2048]{0:T(1024)} %param.12) | copy-start | bytes 24580
  242.4 28.3 %collective-permute-start.9 = (bf16[128,2048]{1,0:T(8,128)(2,1)S(1)}, bf16[128,2048]{1,0:T(8,128)(2,1)S(1)}, u32[]{:S(2)}, u32[]{:S(2)}) collective-permute-start(bf16[128,2048]{1,0:T(8,128)(2,1)S(1)} %add_convert_fusion), channel_id=1, source_target_pairs={{0,8},{8,0},{16,24},{24,16},{32,40},{40,32},{48,56},{56,48},{64,72... | collective-permute-start | bytes 1572872 | tf_op jit(solution)/shard_map/ppermute | solution.py:16
  261.9 8.8 %collective-permute-start.10 = (f32[128]{0:T(128)S(1)}, f32[128]{0:T(128)S(1)}, u32[]{:S(2)}, u32[]{:S(2)}) collective-permute-start(f32[128]{0:T(128)S(1)} %add_rsqrt_fusion), channel_id=1, source_target_pairs={{0,8},{8,0},{16,24},{24,16},{32,40},{40,32},{48,56},{56,48},{64,72... | collective-permute-start | bytes 1544 | tf_op jit(solution)/shard_map/ppermute | solution.py:16
  268.1 7.5 %copy-start.10 = (s32[1024]{0:T(1024)S(1)}, s32[1024]{0:T(1024)}, u32[]{:S(2)}) copy-start(s32[1024]{0:T(1024)} %param.8) | copy-start | bytes 12292
  268.1 7.9 %collective-permute-start.8 = (f32[4,128,250]{2,1,0:T(8,128)S(1)}, f32[4,128,250]{2,1,0:T(8,128)S(1)}, u32[]{:S(2)}, u32[]{:S(2)}) collective-permute-start(f32[4,128,250]{2,1,0:T(8,128)S(1)} %convolution_bitcast_fusion.1), channel_id=1, source_target_pairs={{0,4},{4,0},{1,5},{5,1},{2,6},{6,2},{3,7},{7,3},{8,12},{12,8},{9,1... | collective-permute-start | bytes 1536008 | tf_op jit(solution)/shard_map/ppermute | solution.py:40
  273.7 3.8 %collective-permute-start.11 = (f32[4,128,250]{2,1,0:T(8,128)S(1)}, f32[4,128,250]{2,1,0:T(8,128)S(1)}, u32[]{:S(2)}, u32[]{:S(2)}) collective-permute-start(f32[4,128,250]{2,1,0:T(8,128)S(1)} %convolution_bitcast_fusion), channel_id=1, source_target_pairs={{0,4},{4,0},{1,5},{5,1},{2,6},{6,2},{3,7},{7,3},{8,12},{12,8},{9,1... | collective-permute-start | bytes 1536008 | tf_op jit(solution)/shard_map/ppermute | solution.py:40
  278.9 32.3 %all-to-all-start.1 = ((f32[32,1,24]{2,1,0:T(1,128)}), f32[32,1,24]{2,1,0:T(1,128)S(1)}, u32[]{:S(2)}, u32[]{:S(2)}) async-start(f32[32,1,24]{2,1,0:T(1,128)} %bitcast.15), calls=%async_computation.1 | async-start | bytes 32768 | tf_op jit(solution)/shard_map/all_to_all | solution.py:139

commit v3 on v2

--- a/solution.py
+++ b/solution.py
@@ -90,9 +90,10 @@
     length = lax.psum(sum(jnp.sum(jnp.abs(p.astype(jnp.float32)), axis=1) for p in parts), "row")
     reach = jnp.square(GATE_UP_REACH * length) * (DOWN_REACH * units * grid)
     reach = jnp.maximum(reach, 1e-20) / 30000.0
-    share = (1.0 / reach)[:, None]
     half = own.shape[0]
 
+    parts[2], reach = lax.optimization_barrier((parts[2], reach))
+    share = (1.0 / reach)[:, None]
     gate_part = summed_products(
         parts, [block[:units], after[:units], far_first[:units], before[:units]]
     )
@@ -106,11 +107,15 @@
     downs = [block[units : 2 * units], after[units : 2 * units], far_down, before[units : 2 * units]]
     branch = [jnp.dot(hidden, w, preferred_element_type=jnp.float32) for w in downs]
     branch_other, branch_own = (
-        jnp.concatenate(turned([p[side] for p in branch], "rep", -1), axis=1) * share[side]
+        [p * share[side] for p in turned([p[side] for p in branch], "rep", -1)]
         for side in (slice(0, half), slice(half, 2 * half))
     )
-    arrived = swapped_in_pairs(branch_other.astype(jnp.float16), "grid")
-    pair_sum = (branch_own + arrived.astype(jnp.float32)).astype(jnp.float16)
+    sums = []
+    for step, blocks_of in ((1, slice(0, rep // 2)), (-1, slice(rep // 2, rep))):
+        leaving = jnp.concatenate(branch_other[blocks_of], axis=1).astype(jnp.float16)
+        arrived = shifted(leaving, "grid", step)
+        sums.append(jnp.concatenate(branch_own[blocks_of], axis=1) + arrived.astype(jnp.float32))
+    pair_sum = jnp.concatenate(sums, axis=1).astype(jnp.float16)
     branch = lax.psum(pair_sum, "grid", axis_index_groups=parity_groups(grid))
     mixed_own = (own.astype(jnp.float32) + branch.astype(jnp.float32) * reach[half:, None]).astype(
         jnp.bfloat16

time: 313 us -> 271 us (0.87)
  the two profiles are of different devices: /device:TPU:33 before, /device:TPU:34 now
where the time goes in v3:
time: 271 us; the launch traced here: 270 us
  blocking collectives  111 us (41%)
  starting transfers between devices  95.5 us (35%)
  waiting for transfers between devices  30.1 us (11%)
  matrix products  16.4 us (6%)
  local copies, waits for them, and re-layouts  8.29 us (3%)
  other arithmetic  7.25 us (3%)
    psum x1, blocking collectives, device_step(): branch = lax.psum(pair_sum, 'grid', axis_index_groups=parity_groups(grid))  68.4 us
    ppermute x6, starting transfers between devices, shifted(): lax.ppermute(value, axis, [(i, (i + step) % size) for i in range(size)])  56.3 us
    all_gather x1, blocking collectives, device_step(): lax.all_gather(tokens, 'grid', axis=0, axis_index_groups=parity_groups(gr...  37.6 us
    all_to_all x1, waiting for transfers between devices, device_step(): lax.all_to_all(pieces, 'grid', 0, 0, tiled=True).reshape(grid, 3, own_rows)  21 us
    all_to_all x1, starting transfers between devices, device_step(): lax.all_to_all(pieces, 'grid', 0, 0, tiled=True).reshape(grid, 3, own_rows)  12.5 us
    ppermute x3, starting transfers between devices, swapped_in_pairs(): return lax.ppermute(value, axis, [(i, i ^ 1) for i in range(size)])  9.75 us
    ppermute x4, starting transfers between devices, both_halves(): return part + lax.ppermute(part, axis, [(0, 1), (1, 0)])  8.91 us
    dot_general x8, matrix products, summed_products(): lax.dot_general(p, w, (((1,), (1,)), ((), ())), preferred_element_type=jn...  8.2 us
  transfers between devices with their start and end apart: 15, of which 4 were waited for; matrix products, arithmetic and copies ran while one was open for 10% of the time, Pallas kernels for 0%

profile of v3, /device:TPU:34, one launch (start us, length us, event | category | flops | bytes accessed | tf_op | source)
XLA Modules:
  0.0 269.8 jit_solution(15137453486104695370)
XLA Ops:
  0.6 1.4 pad_maximum_fusion
  2.0 42.3 %collective-permute-start = (bf16[1344,512]{1,0:T(8,128)(2,1)S(1)}, bf16[1344,512]{1,0:T(8,128)(2,1)S(1)}, u32[]{:S(2)}, u32[]{:S(2)}) collective-permute-start(bf16[1344,512]{1,0:T(8,128)(2,1)S(1)} %pad_maximum_fusion), channel_id=1, source_target_pairs={{0,3},{1,0},{2,1},{3,2},{4,7},{5,4},{6,5},{7,6},{8,11},{9,8},{10,9... | collective-permute-start | bytes 4128776 | tf_op jit(solution)/shard_map/ppermute | solution.py:28
  44.4 2.0 collective-permute-start.1
  46.4 37.6 %all-gather = bf16[128,2048]{1,0:T(8,128)(2,1)S(1)} all-gather(bf16[8,2048]{1,0:T(8,128)(2,1)S(1)} %copy-done.8), channel_id=2, replica_groups={{0,16,32,48,64,80,96,112,128,144,160,176,192,208,224,240},{8,24,40,56,7..., dimensions={0}, use_global_device_ids=true | all-gather | bytes 557056 | tf_op jit(solution)/shard_map/all_gather | solution.py:76
  84.0 3.9 %collective-permute-start.2 = (bf16[128,2048]{1,0:T(8,128)(2,1)S(1)}, bf16[128,2048]{1,0:T(8,128)(2,1)}, u32[]{:S(2)}, u32[]{:S(2)}) collective-permute-start(bf16[128,2048]{1,0:T(8,128)(2,1)S(1)} %all-gather), channel_id=1, source_target_pairs={{0,8},{8,0},{16,24},{24,16},{32,40},{40,32},{48,56},{56,48},{64,72... | collective-permute-start | bytes 1572872 | tf_op jit(solution)/shard_map/ppermute | solution.py:16
  87.8 0.9 slice.92
  88.7 3.6 %collective-permute-start.5 = (bf16[672,512]{1,0:T(8,128)(2,1)}, bf16[672,512]{1,0:T(8,128)(2,1)}, u32[]{:S(2)}, u32[]{:S(2)}) collective-permute-start(bf16[672,512]{1,0:T(8,128)(2,1)} %slice.92), channel_id=1, source_target_pairs={{0,1},{1,2},{2,3},{3,0},{4,5},{5,6},{6,7},{7,4},{8,9},{9,10},{10,1... | collective-permute-start | bytes 2064392 | tf_op jit(solution)/shard_map/ppermute | solution.py:28
  92.3 0.9 slice.88
  93.2 2.5 collective-permute-start.3
  95.8 1.2 select_select_fusion.3
  97.0 2.2 fusion.27
  99.2 0.2 abs_reduce_fusion
  99.4 0.3 fusion.33
  99.7 0.2 abs_reduce_fusion.2
  99.9 1.1 convolution_add_fusion.1
  101.0 2.5 psum.21
  103.5 1.3 fusion.30
  104.9 0.3 fusion.34
  105.2 0.3 convolution_add_fusion.3
  105.5 0.3 copy-done.3
  105.9 0.1 copy-done.6
  106.0 1.3 fusion
  107.4 2.2 collective-permute-start.6
  109.6 1.3 fusion.1
  111.0 2.3 collective-permute-start.4
  113.3 2.2 broadcast_in_dim.6
  115.5 8.1 %all-to-all-start = ((bf16[4,2048,250]{2,1,0:T(8,128)(2,1)}), bf16[4,2048,250]{2,1,0:T(8,128)(2,1)}, u32[]{:S(2)}, u32[]{:S(2)}) async-start(bf16[4,2048,250]{2,1,0:T(8,128)(2,1)} %broadcast_in_dim.6), calls=%async_computation | async-start | bytes 8388608 | tf_op jit(solution)/shard_map/all_to_all | solution.py:21
  123.6 1.0 slice.118
  124.5 1.0 slice.117
  125.5 1.3 multiply_convert_fusion.1
  126.8 0.3 fusion.23
  127.2 1.3 fusion.25
  128.5 0.3 fusion.48
  128.8 0.3 fusion.19
  129.2 0.2 multiply_convert_fusion.5
  129.3 0.1 multiply_convert_fusion.2
  129.6 3.3 %collective-permute-start.8 = (f16[128,1024]{1,0:T(8,128)(2,1)S(1)}, f16[128,1024]{1,0:T(8,128)(2,1)S(1)}, u32[]{:S(2)}, u32[]{:S(2)}) collective-permute-start(f16[128,1024]{1,0:T(8,128)(2,1)S(1)} %pad_maximum_fusion.7), channel_id=1, source_target_pairs={{0,248},{8,0},{16,8},{24,16},{32,24},{40,32},{48,40},{56,48},{64,5... | collective-permute-start | bytes 786440 | tf_op jit(solution)/shard_map/ppermute | solution.py:28
  132.9 2.6 collective-permute-start.7
  135.5 0.1 select_multiply_fusion.3
  135.7 3.9 %collective-permute-done.8 = f16[128,1024]{1,0:T(8,128)(2,1)S(1)} collective-permute-done((f16[128,1024]{1,0:T(8,128)(2,1)S(1)}, f16[128,1024]{1,0:T(8,128)(2,1)S(1)}, u32[]{:S(2)}, u32[]{:S(2)}) %collective-permute-start.8) | collective-permute-done | bytes 262176 | tf_op jit(solution)/shard_map/ppermute | solution.py:28
  139.6 4.2 %collective-permute-done.7 = f16[128,1024]{1,0:T(8,128)(2,1)S(1)} collective-permute-done((f16[128,1024]{1,0:T(8,128)(2,1)S(1)}, f16[128,1024]{1,0:T(8,128)(2,1)S(1)}, u32[]{:S(2)}, u32[]{:S(2)}) %collective-permute-start.7) | collective-permute-done | bytes 262176 | tf_op jit(solution)/shard_map/ppermute | solution.py:28
  143.9 0.1 pad_maximum_fusion.1
  144.1 68.4 %all-reduce.1 = u32[4,32768]{1,0:T(4,128)S(1)} all-reduce(u32[4,32768]{1,0:T(4,128)S(1)} %bitcast.53), channel_id=1, replica_groups={{0,16,32,48,64,80,96,112,128,144,160,176,192,208,224,240},{8,24,40,56,7..., use_global_device_ids=true, to_apply=%region_5.6.clone | all-reduce | flops 131072 | bytes 1048576 | tf_op jit(solution)/shard_map/psum | solution.py:119
  212.5 0.2 add_convert_fusion
  212.8 2.1 collective-permute-start.10
  214.9 0.2 fusion.2
  215.0 2.5 psum.23
  217.6 3.8 %collective-permute-start.11 = (f32[128]{0:T(128)S(1)}, f32[128]{0:T(128)S(1)}, u32[]{:S(2)}, u32[]{:S(2)}) collective-permute-start(f32[128]{0:T(128)S(1)} %add_rsqrt_fusion), channel_id=1, source_target_pairs={{0,8},{8,0},{16,24},{24,16},{32,40},{40,32},{48,56},{56,48},{64,72... | collective-permute-start | bytes 1544 | tf_op jit(solution)/shard_map/ppermute | solution.py:16
  221.4 2.9 %convolution_bitcast_fusion.1 = f32[4,128,250]{2,1,0:T(8,128)S(1)} fusion(bf16[4,2048,250]{2,1,0:T(8,128)(2,1)} %all-to-all-done, bf16[128,2048]{1,0:T(8,128)(2,1)S(1)} %add_convert_fusion, f32[2048]{0:T(1024)S(1)} %copy-done.7, f32[128]{0:T(128)S(1)} %add_rsqrt_fusion), kind=kOutput, calls=%fused_computation.4 | convolution fusion | flops 525336576 | bytes 5140992 | tf_op jit(solution)/shard_map/tk,rkv->rtv/dot_general | solution.py:51
  224.4 2.0 collective-permute-start.9
  226.4 2.9 %convolution_bitcast_fusion = f32[4,128,250]{2,1,0:T(8,128)S(1)} fusion(bf16[4,2048,250]{2,1,0:T(8,128)(2,1)} %all-to-all-done, bf16[128,2048]{1,0:T(8,128)(2,1)S(1)} %collective-permute-done.10, f32[128]{0:T(128)S(1)} %collective-permute-done.11, f32[2048]{0:T(1024)S(1)} %copy-done.7), kind=kOutput, calls=%fused_computation.3 | convolution fusion | flops 525336576 | bytes 5140992 | tf_op jit(solution)/shard_map/tk,rkv->rtv/dot_general | solution.py:51
  229.3 2.4 collective-permute-start.12
  231.8 0.1 reshape.54
  232.2 0.1 fusion.45
  232.3 0.9 collective-permute-done.12
  233.3 0.1 fusion.46
  233.4 0.4 exponential_reduce_fusion.1
  234.0 0.7 all_to_all.10
  234.7 12.5 %all-to-all-start.1 = ((f32[32,1,24]{2,1,0:T(1,128)}), f32[32,1,24]{2,1,0:T(1,128)S(1)}, u32[]{:S(2)}, u32[]{:S(2)}) async-start(f32[32,1,24]{2,1,0:T(1,128)} %bitcast.15), calls=%async_computation.1 | async-start | bytes 32768 | tf_op jit(solution)/shard_map/all_to_all | solution.py:144
  247.2 0.6 constant_dynamic-slice_fusion
  247.8 21.0 %all-to-all-done.1 = f32[32,1,24]{2,1,0:T(1,128)S(1)} async-done(((f32[32,1,24]{2,1,0:T(1,128)}), f32[32,1,24]{2,1,0:T(1,128)S(1)}, u32[]{:S(2)}, u32[]{:S(2)}) %all-to-all-start.1) | async-done | bytes 3104 | tf_op jit(solution)/shard_map/all_to_all | solution.py:144
  268.9 0.2 slice_reduce_fusion
  269.1 0.2 fusion.36
  269.3 0.5 log_subtract_fusion
  (53 shorter events, 0.9 us)
Async XLA Ops:
  0.6 45.7 %copy-start.8 = (bf16[8,2048]{1,0:T(8,128)(2,1)S(1)}, bf16[8,2048]{1,0:T(8,128)(2,1)}, u32[]{:S(2)}) copy-start(bf16[8,2048]{1,0:T(8,128)(2,1)} %param.7) | copy-start | bytes 98308
  2.0 81.9 %collective-permute-start = (bf16[1344,512]{1,0:T(8,128)(2,1)S(1)}, bf16[1344,512]{1,0:T(8,128)(2,1)S(1)}, u32[]{:S(2)}, u32[]{:S(2)}) collective-permute-start(bf16[1344,512]{1,0:T(8,128)(2,1)S(1)} %pad_maximum_fusion), channel_id=1, source_target_pairs={{0,3},{1,0},{2,1},{3,2},{4,7},{5,4},{6,5},{7,6},{8,11},{9,8},{10,9... | collective-permute-start | bytes 4128776 | tf_op jit(solution)/shard_map/ppermute | solution.py:28
  44.4 39.6 %collective-permute-start.1 = (bf16[1344,512]{1,0:T(8,128)(2,1)S(1)}, bf16[1344,512]{1,0:T(8,128)(2,1)S(1)}, u32[]{:S(2)}, u32[]{:S(2)}) collective-permute-start(bf16[1344,512]{1,0:T(8,128)(2,1)S(1)} %pad_maximum_fusion), channel_id=1, source_target_pairs={{0,1},{1,2},{2,3},{3,0},{4,5},{5,6},{6,7},{7,4},{8,9},{9,10},{10,1... | collective-permute-start | bytes 4128776 | tf_op jit(solution)/shard_map/ppermute | solution.py:28
  84.0 9.2 %copy-start.5 = (bf16[1344,512]{1,0:T(8,128)(2,1)}, bf16[1344,512]{1,0:T(8,128)(2,1)S(1)}, u32[]{:S(2)}) copy-start(bf16[1344,512]{1,0:T(8,128)(2,1)S(1)} %collective-permute-done.1) | copy-start | bytes 4128772
  84.0 11.8 %collective-permute-start.2 = (bf16[128,2048]{1,0:T(8,128)(2,1)S(1)}, bf16[128,2048]{1,0:T(8,128)(2,1)}, u32[]{:S(2)}, u32[]{:S(2)}) collective-permute-start(bf16[128,2048]{1,0:T(8,128)(2,1)S(1)} %all-gather), channel_id=1, source_target_pairs={{0,8},{8,0},{16,24},{24,16},{32,40},{40,32},{48,56},{56,48},{64,72... | collective-permute-start | bytes 1572872 | tf_op jit(solution)/shard_map/ppermute | solution.py:16
  88.7 16.8 %collective-permute-start.5 = (bf16[672,512]{1,0:T(8,128)(2,1)}, bf16[672,512]{1,0:T(8,128)(2,1)}, u32[]{:S(2)}, u32[]{:S(2)}) collective-permute-start(bf16[672,512]{1,0:T(8,128)(2,1)} %slice.92), channel_id=1, source_target_pairs={{0,1},{1,2},{2,3},{3,0},{4,5},{5,6},{6,7},{7,4},{8,9},{9,10},{10,1... | collective-permute-start | bytes 2064392 | tf_op jit(solution)/shard_map/ppermute | solution.py:28
  93.2 16.4 %collective-permute-start.3 = (bf16[672,512]{1,0:T(8,128)(2,1)}, bf16[672,512]{1,0:T(8,128)(2,1)}, u32[]{:S(2)}, u32[]{:S(2)}) collective-permute-start(bf16[672,512]{1,0:T(8,128)(2,1)} %slice.88), channel_id=1, source_target_pairs={{0,3},{1,0},{2,1},{3,2},{4,7},{5,4},{6,5},{7,6},{8,11},{9,8},{10,9... | collective-permute-start | bytes 2064392 | tf_op jit(solution)/shard_map/ppermute | solution.py:28
  97.0 2.4 copy-start
  99.9 5.0 %copy-start.1 = (bf16[512,448]{0,1:T(8,128)(2,1)S(1)}, bf16[512,448]{0,1:T(8,128)(2,1)}, u32[]{:S(2)}) copy-start(bf16[512,448]{0,1:T(8,128)(2,1)} %param.9) | copy-start | bytes 1376260
  104.9 1.0 copy-start.3
  104.9 1.1 copy-start.6
  107.3 5.9 %copy-start.4 = (bf16[2048,250]{1,0:T(8,128)(2,1)S(1)}, bf16[2048,250]{1,0:T(8,128)(2,1)}, u32[]{:S(2)}) copy-start(bf16[2048,250]{1,0:T(8,128)(2,1)} %param.13) | copy-start | bytes 3072004
  107.4 18.1 %collective-permute-start.6 = (f32[256,448]{0,1:T(8,128)S(1)}, f32[256,448]{0,1:T(8,128)}, u32[]{:S(2)}, u32[]{:S(2)}) collective-permute-start(f32[256,448]{0,1:T(8,128)S(1)} %fusion), channel_id=1, source_target_pairs={{0,4},{4,0},{1,5},{5,1},{2,6},{6,2},{3,7},{7,3},{8,12},{12,8},{9,1... | collective-permute-start | bytes 1376264 | tf_op jit(solution)/shard_map/ppermute | solution.py:40
  111.0 14.5 %collective-permute-start.4 = (f32[256,448]{0,1:T(8,128)S(1)}, f32[256,448]{0,1:T(8,128)}, u32[]{:S(2)}, u32[]{:S(2)}) collective-permute-start(f32[256,448]{0,1:T(8,128)S(1)} %fusion.1), channel_id=1, source_target_pairs={{0,4},{4,0},{1,5},{5,1},{2,6},{6,2},{3,7},{7,3},{8,12},{12,8},{9,1... | collective-permute-start | bytes 1376264 | tf_op jit(solution)/shard_map/ppermute | solution.py:40
  115.5 105.9 %all-to-all-start = ((bf16[4,2048,250]{2,1,0:T(8,128)(2,1)}), bf16[4,2048,250]{2,1,0:T(8,128)(2,1)}, u32[]{:S(2)}, u32[]{:S(2)}) async-start(bf16[4,2048,250]{2,1,0:T(8,128)(2,1)} %broadcast_in_dim.6), calls=%async_computation | async-start | bytes 8388608 | tf_op jit(solution)/shard_map/all_to_all | solution.py:21
  126.8 1.7 copy-start.2
  129.6 10.0 %collective-permute-start.8 = (f16[128,1024]{1,0:T(8,128)(2,1)S(1)}, f16[128,1024]{1,0:T(8,128)(2,1)S(1)}, u32[]{:S(2)}, u32[]{:S(2)}) collective-permute-start(f16[128,1024]{1,0:T(8,128)(2,1)S(1)} %pad_maximum_fusion.7), channel_id=1, source_target_pairs={{0,248},{8,0},{16,8},{24,16},{32,24},{40,32},{48,40},{56,48},{64,5... | collective-permute-start | bytes 786440 | tf_op jit(solution)/shard_map/ppermute | solution.py:28
  132.9 10.9 %collective-permute-start.7 = (f16[128,1024]{1,0:T(8,128)(2,1)S(1)}, f16[128,1024]{1,0:T(8,128)(2,1)S(1)}, u32[]{:S(2)}, u32[]{:S(2)}) collective-permute-start(f16[128,1024]{1,0:T(8,128)(2,1)S(1)} %pad_maximum_fusion.6), channel_id=1, source_target_pairs={{0,8},{8,16},{16,24},{24,32},{32,40},{40,48},{48,56},{56,64},{64,7... | collective-permute-start | bytes 786440 | tf_op jit(solution)/shard_map/ppermute | solution.py:28
  144.1 77.3 %copy-start.7 = (f32[2048]{0:T(1024)S(1)}, f32[2048]{0:T(1024)}, u32[]{:S(2)}) copy-start(f32[2048]{0:T(1024)} %param.12) | copy-start | bytes 24580
  212.8 13.6 %collective-permute-start.10 = (bf16[128,2048]{1,0:T(8,128)(2,1)S(1)}, bf16[128,2048]{1,0:T(8,128)(2,1)S(1)}, u32[]{:S(2)}, u32[]{:S(2)}) collective-permute-start(bf16[128,2048]{1,0:T(8,128)(2,1)S(1)} %add_convert_fusion), channel_id=1, source_target_pairs={{0,8},{8,0},{16,24},{24,16},{32,40},{40,32},{48,56},{56,48},{64,72... | collective-permute-start | bytes 1572872 | tf_op jit(solution)/shard_map/ppermute | solution.py:16
  217.6 8.8 %collective-permute-start.11 = (f32[128]{0:T(128)S(1)}, f32[128]{0:T(128)S(1)}, u32[]{:S(2)}, u32[]{:S(2)}) collective-permute-start(f32[128]{0:T(128)S(1)} %add_rsqrt_fusion), channel_id=1, source_target_pairs={{0,8},{8,0},{16,24},{24,16},{32,40},{40,32},{48,56},{56,48},{64,72... | collective-permute-start | bytes 1544 | tf_op jit(solution)/shard_map/ppermute | solution.py:16
  224.4 7.4 %copy-start.9 = (s32[1024]{0:T(1024)S(1)}, s32[1024]{0:T(1024)}, u32[]{:S(2)}) copy-start(s32[1024]{0:T(1024)} %param.8) | copy-start | bytes 12292
  224.4 7.8 %collective-permute-start.9 = (f32[4,128,250]{2,1,0:T(8,128)S(1)}, f32[4,128,250]{2,1,0:T(8,128)S(1)}, u32[]{:S(2)}, u32[]{:S(2)}) collective-permute-start(f32[4,128,250]{2,1,0:T(8,128)S(1)} %convolution_bitcast_fusion.1), channel_id=1, source_target_pairs={{0,4},{4,0},{1,5},{5,1},{2,6},{6,2},{3,7},{7,3},{8,12},{12,8},{9,1... | collective-permute-start | bytes 1536008 | tf_op jit(solution)/shard_map/ppermute | solution.py:40
  229.3 4.0 %collective-permute-start.12 = (f32[4,128,250]{2,1,0:T(8,128)S(1)}, f32[4,128,250]{2,1,0:T(8,128)S(1)}, u32[]{:S(2)}, u32[]{:S(2)}) collective-permute-start(f32[4,128,250]{2,1,0:T(8,128)S(1)} %convolution_bitcast_fusion), channel_id=1, source_target_pairs={{0,4},{4,0},{1,5},{5,1},{2,6},{6,2},{3,7},{7,3},{8,12},{12,8},{9,1... | collective-permute-start | bytes 1536008 | tf_op jit(solution)/shard_map/ppermute | solution.py:40
  234.7 34.1 %all-to-all-start.1 = ((f32[32,1,24]{2,1,0:T(1,128)}), f32[32,1,24]{2,1,0:T(1,128)S(1)}, u32[]{:S(2)}, u32[]{:S(2)}) async-start(f32[32,1,24]{2,1,0:T(1,128)} %bitcast.15), calls=%async_computation.1 | async-start | bytes 32768 | tf_op jit(solution)/shard_map/all_to_all | solution.py:144
